TPU v7x, 32 devices: a whole 2x2x4 slice. The times are simulated.
32 devices in a mesh: slab: 16 (over z, x, core), layer: 2 (over y).
Axes of the slice: x: 2, y: 2, z: 4, core: 2. Of those that a mesh axis runs over, the one named last changes fastest.
Arguments:
- nodal_field: float32 [2, 1024, 4, 4, 512], P('layer', 'slab'), may hold values from -6 to 6
- metric: float32 [2, 1024, 4, 4, 3, 512], P('layer', 'slab'), may hold values from 0.25 to 2
- slab_ids: int32 [1024], replicated, may hold values from 0 to 1023, as said below
- face_map: int32 [1024, 1024], P('slab'), may hold values from 0 to 1023, as said below
Outputs:
- assembled: float32 [2, 1024, 4, 4, 512], P('layer', 'slab')
Inputs may be any that keep to these rules, and one draw needn't show every extreme that they name: slab_ids is a permutation of 0 to 1023; positions p of one device are those with p // 64 equal to its index along slab, and for one rotation R every device holds exactly the slabs g with (g + R) mod 16 equal to its index, in any order of its positions, so slab (g + 1) mod 1024 always sits on the next device along slab, cyclically. Each row of face_map is a permutation of 0 to 1023: either the identity, or the map that reverses y, sending (ez, ey, c, b) to (ez, 3 - ey, c, 7 - b); z order is never changed.
All inputs are finite; a program needn't handle non-finite values.
Results may differ from a plain program's by a relative error of at most 0.00005.
Values sent between devices are 32-bit elements; how exact they have to be, the bound alone decides.
No kernel may reach another device: no remote copies, remote signals or barrier semaphores. Data moves between devices by JAX's collectives and lax.ppermute only.
A program may use at most 192 MiB of HBM per device.

v0:
```python
import jax
import jax.numpy as jnp
import numpy as np
from jax import lax
from jax.sharding import PartitionSpec as P

P_SIZE = 8
PTS = 512
EY = 4
EZ = 4
FACE = 1024


def from_behind(array, axis, by):
    peers = lax.axis_size(axis)
    return lax.ppermute(array, axis, [(i, (i + by) % peers) for i in range(peers)])


def from_partner(value, axis, apart):
    mask = 2**apart
    pairs = [(source, source ^ mask) for source in range(lax.axis_size(axis))]
    return lax.ppermute(value, axis, pairs)


def legendre_pair(gll_nodes, degree):
    lower_poly = gll_nodes * 0.0 + 1.0
    upper_poly = gll_nodes.copy()
    for poly_order in range(2, degree + 1):
        lower_poly, upper_poly = (
            upper_poly,
            ((2 * poly_order - 1) * gll_nodes * upper_poly - (poly_order - 1) * lower_poly)
            / poly_order,
        )
    return (lower_poly, upper_poly)


def gll_tables():
    degree = P_SIZE - 1
    gll_nodes = -np.cos(np.pi * np.arange(P_SIZE) / degree)
    for newton_sweep in range(100):
        lower_poly, upper_poly = legendre_pair(gll_nodes, degree)
        gll_nodes = gll_nodes - (gll_nodes * upper_poly - lower_poly) / ((degree + 1) * upper_poly)
    lower_poly, upper_poly = legendre_pair(gll_nodes, degree)
    quad_weights = 2.0 / (degree * (degree + 1) * upper_poly * upper_poly)
    identity = np.eye(P_SIZE)
    differ = gll_nodes[:, None] - gll_nodes[None, :] + identity
    derivative = upper_poly[:, None] / (upper_poly[None, :] * differ)
    derivative = derivative * (1.0 - identity)
    derivative[0, 0] = -degree * (degree + 1) / 4.0
    derivative[degree, degree] = degree * (degree + 1) / 4.0
    weight_cube = (
        quad_weights[:, None, None] * quad_weights[None, :, None] * quad_weights[None, None, :]
    )
    identity_two = np.kron(identity, identity)
    along_x = np.kron(identity_two, derivative)
    along_y = np.kron(identity, np.kron(derivative, identity))
    along_z = np.kron(derivative, identity_two)
    operator_stack = np.concatenate([along_x, along_y, along_z], 0)
    weight_rows = np.tile(weight_cube.reshape(-1), 3)
    return (jnp.asarray(operator_stack, jnp.float32), jnp.asarray(weight_rows, jnp.float32))


def local_apply(values, factors, operator_stack, weight_rows):
    highest = lax.Precision.HIGHEST
    gradients = jnp.dot(
        values, operator_stack.T, precision=highest, preferred_element_type=jnp.float32
    )
    fluxes = gradients * (weight_rows * factors)
    result = jnp.dot(fluxes, operator_stack, precision=highest, preferred_element_type=jnp.float32)
    return result.reshape(values.shape[:-1] + (P_SIZE, P_SIZE, P_SIZE))


def assemble_slab(values):
    low_plane = values[..., :, :, :, 0:1, :]
    high_plane = values[..., :, :, :, P_SIZE - 1 : P_SIZE, :]
    zero_plane = jnp.zeros_like(low_plane[..., :, 0:1, :, :, :])
    from_after = jnp.concatenate([low_plane[..., :, 1:, :, :, :], zero_plane], axis=-4)
    from_before = jnp.concatenate([zero_plane, high_plane[..., :, :-1, :, :, :]], axis=-4)
    b_iota = jnp.arange(P_SIZE)[:, None]
    values = (
        values
        + jnp.where(b_iota == P_SIZE - 1, from_after, 0.0)
        + jnp.where(b_iota == 0, from_before, 0.0)
    )
    low_plane = values[..., :, :, 0:1, :, :]
    high_plane = values[..., :, :, P_SIZE - 1 : P_SIZE, :, :]
    zero_plane = jnp.zeros_like(low_plane[..., 0:1, :, :, :, :])
    from_after = jnp.concatenate([low_plane[..., 1:, :, :, :, :], zero_plane], axis=-5)
    from_before = jnp.concatenate([zero_plane, high_plane[..., :-1, :, :, :, :]], axis=-5)
    c_iota = jnp.arange(P_SIZE)[:, None, None]
    values = (
        values
        + jnp.where(c_iota == P_SIZE - 1, from_after, 0.0)
        + jnp.where(c_iota == 0, from_before, 0.0)
    )
    return values


def face_of(local_out, column):
    return local_out[..., column].reshape(local_out.shape[:-5] + (FACE,))


def put_faces(local_out, left_values, right_values):
    inner_shape = local_out.shape[:-1] + (1,)
    return jnp.concatenate(
        [
            left_values.reshape(inner_shape),
            local_out[..., 1 : P_SIZE - 1],
            right_values.reshape(inner_shape),
        ],
        axis=-1,
    )


def flip_face(face_values):
    grid = face_values.reshape(face_values.shape[:-1] + (EZ, EY, P_SIZE, P_SIZE))
    grid = jnp.flip(jnp.flip(grid, -3), -1)
    return grid.reshape(face_values.shape)


def reorient(face_values, flipped):
    return jnp.where(flipped, flip_face(face_values), face_values)


def reorient_edge(edge_values, flipped):
    return jnp.where(flipped, jnp.flip(edge_values, -1), edge_values)


def pick_rows(selector, rows):
    return jnp.einsum("st,...tf->...sf", selector, rows, precision=lax.Precision.HIGHEST)


def body(nodal_field, metric, slab_ids, face_map):
    operator_stack, weight_rows = gll_tables()
    slab_count = nodal_field.shape[1]
    cycle_size = lax.axis_size("slab")
    total_slabs = slab_count * cycle_size
    device = lax.axis_index("slab")
    values = nodal_field.reshape(slab_count, EZ, EY, PTS)
    factors = metric.reshape(slab_count, EZ, EY, 3 * PTS)
    flipped = face_map[:, 0:1] != 0
    local_out = assemble_slab(local_apply(values, factors, operator_stack, weight_rows))
    right_face = face_of(local_out, P_SIZE - 1)
    left_face = face_of(local_out, 0)
    from_prev = from_behind(reorient(right_face, flipped), "slab", 1)
    from_next = from_behind(left_face, "slab", -1)
    own_ids = lax.dynamic_slice_in_dim(slab_ids, device * slab_count, slab_count)
    prev_ids = lax.dynamic_slice_in_dim(
        slab_ids, (device + cycle_size - 1) % cycle_size * slab_count, slab_count
    )
    next_ids = lax.dynamic_slice_in_dim(
        slab_ids, (device + 1) % cycle_size * slab_count, slab_count
    )
    want_prev = (own_ids + total_slabs - 1) % total_slabs
    want_next = (own_ids + 1) % total_slabs
    prev_select = (prev_ids[None, :] == want_prev[:, None]).astype(jnp.float32)
    next_select = (next_ids[None, :] == want_next[:, None]).astype(jnp.float32)
    left_sum = left_face + pick_rows(prev_select, from_prev)
    right_sum = right_face + reorient(pick_rows(next_select, from_next), flipped)
    ez_iota = jnp.arange(EZ)[:, None, None, None, None]
    c_iota = jnp.arange(P_SIZE)[None, None, :, None, None]
    bottom_mask = (ez_iota == 0) & (c_iota == 0)
    top_mask = (ez_iota == EZ - 1) & (c_iota == P_SIZE - 1)
    raw_top = local_out[:, EZ - 1, :, P_SIZE - 1, :, :].reshape(slab_count, EY * P_SIZE * P_SIZE)
    raw_bottom = local_out[:, 0, :, 0, :, :].reshape(slab_count, EY * P_SIZE * P_SIZE)
    partner = from_partner(jnp.stack([raw_bottom, raw_top], 0), "layer", 0)
    edge_grid = partner.reshape(2, slab_count, EY, P_SIZE, P_SIZE)
    far_right = edge_grid[..., P_SIZE - 1].reshape(2, slab_count, EY * P_SIZE)
    far_left = edge_grid[..., 0].reshape(2, slab_count, EY * P_SIZE)
    sent_right = reorient_edge(far_right, flipped[None])
    edges_prev = from_behind(sent_right, "slab", 1)
    edges_next = from_behind(far_left, "slab", -1)
    diag_left = pick_rows(prev_select, edges_prev).reshape(2, slab_count, EY, P_SIZE, 1)
    diag_right = reorient_edge(pick_rows(next_select, edges_next), flipped[None]).reshape(
        2, slab_count, EY, P_SIZE, 1
    )
    middle_zero = jnp.zeros((2, slab_count, EY, P_SIZE, P_SIZE - 2), jnp.float32)
    correction = jnp.concatenate([diag_left, middle_zero, diag_right], axis=-1).reshape(
        2, slab_count, EY * P_SIZE * P_SIZE
    )
    local_out = put_faces(local_out, left_sum, right_sum)
    top_face = local_out[:, EZ - 1, :, P_SIZE - 1, :, :].reshape(slab_count, EY * P_SIZE * P_SIZE)
    bottom_face = local_out[:, 0, :, 0, :, :].reshape(slab_count, EY * P_SIZE * P_SIZE)
    bottom_sum = bottom_face + partner[1] + correction[1]
    top_sum = top_face + partner[0] + correction[0]
    bottom_grid = bottom_sum.reshape(slab_count, 1, EY, 1, P_SIZE, P_SIZE)
    top_grid = top_sum.reshape(slab_count, 1, EY, 1, P_SIZE, P_SIZE)
    local_out = jnp.where(bottom_mask, bottom_grid, local_out)
    local_out = jnp.where(top_mask, top_grid, local_out)
    return local_out.reshape(1, slab_count, EZ, EY, PTS)


def solution(mesh):
    return jax.shard_map(
        body,
        mesh=mesh,
        in_specs=(
            P("layer", "slab", None, None, None),
            P("layer", "slab", None, None, None, None),
            P(),
            P("slab", None),
        ),
        out_specs=P("layer", "slab", None, None, None),
        check_vma=False,
    )
```

profile of v0, /device:TPU:0, one launch (start us, length us, event | category | flops | bytes accessed | tf_op | source)
XLA Modules:
  0.0 100.0 jit_solution(5411365979549020003)
XLA Ops:
  0.0 9.4 %copy.18 = f32[1,64,4,4,3,512]{5,4,1,3,2,0:T(4,128)} copy(f32[1,64,4,4,3,512]{5,3,4,2,1,0:T(4,128)} %param.7) | data formatting | bytes 12582912 | tf_op args[1]
  9.4 11.4 %reshape.145 = f32[64,4,4,1536]{3,0,2,1:T(8,128)} reshape(f32[1,64,4,4,3,512]{5,4,1,3,2,0:T(4,128)} %copy.18) | data formatting | bytes 12582912 | tf_op jit(solution)/shard_map/reshape | solution.py:140
  20.8 13.5 %fusion.3 = f32[1536,64,4,4]{0,1,3,2:T(8,128)S(1)} fusion(f32[1536,512,1,1]{1,0,3,2:T(8,128)} %constant.85, f32[64,4,4,512]{3,2,1,0:T(4,128)S(1)} %bitcast.90), kind=kOutput, calls=%fused_computation.8 | convolution fusion | flops 9663676416 | bytes 11534336 | tf_op jit(solution)/shard_map/dot_general | solution.py:65
  34.4 21.0 %fusion = f32[64,4,4,512]{0,3,2,1:T(8,128)S(1)} fusion(f32[1536,512,1,1]{1,0,3,2:T(8,128)S(1)} %copy-done.4, f32[1536,64,4,4]{0,1,3,2:T(8,128)S(1)} %fusion.3, f32[64,4,4,1536]{3,0,2,1:T(8,128)S(1)} %copy-done.3, f32[1536]{0:T(1024)S(1)} %copy-done.5), kind=kOutput, calls=%fused_computation.1 | convolution fusion | flops 9666822144 | bytes 17831936 | tf_op jit(solution)/shard_map/dot_general | solution.py:69
  55.6 1.3 %select_add_fusion.1 = f32[64,4,4,8,8,8]{0,5,4,3,2,1:T(8,128)S(1)} fusion(f32[64,4,4,8,8,8]{0,5,4,3,2,1:T(8,128)S(1)} %bitcast.92, f32[64,4,4,8,8]{0,4,3,2,1:T(8,128)S(1)} %get-tuple-element.25, f32[64,4,4,8,8]{0,4,3,2,1:T(8,128)S(1)} %get-tuple-element.26, pred[8]{0:T(512)(128)(4,1)S(1)} %get-tuple-element.27, pred[8]{0:T(512)(128)(4,1)S(1)} %get-tuple-element.28), kind=kLoop, calls=%fused_computation.6 | loop fusion | flops 2097152 | bytes 4718608 | tf_op jit(solution)/shard_map/add | solution.py:81
  57.0 1.6 %select_add_fusion = f32[64,4,4,8,8,8]{0,5,4,3,2,1:T(8,128)S(1)} fusion(f32[64,4,4,8,8]{0,4,3,2,1:T(8,128)S(1)} %pad_bitcast_fusion, f32[64,4,4,8,8]{0,4,3,2,1:T(8,128)S(1)} %pad_bitcast_fusion.1, pred[8]{0:T(512)(128)(4,1)S(1)} %get-tuple-element.27, pred[8]{0:T(512)(128)(4,1)S(1)} %get-tuple-element.28, f32[64,4,4,8,8]{0,4,3,2,1:T(8,128)S(1)} %get-tuple-element.25, ...), kind=kLoop, calls=%fused_computation.5 | loop fusion | flops 4194304 | bytes 5242896 | tf_op jit(solution)/shard_map/add | solution.py:92
  58.7 3.1 %collective-permute-start.2 = (f32[2,64,256]{1,2,0:T(8,128)S(1)}, f32[2,64,256]{1,2,0:T(8,128)S(1)}, u32[]{:S(2)}, u32[]{:S(2)}) collective-permute-start(f32[2,64,256]{1,2,0:T(8,128)S(1)} %pad_maximum_fusion.1), channel_id=1, source_target_pairs={{0,1},{1,0},{2,3},{3,2},{4,5},{5,4},{6,7},{7,6},{8,9},{9,8},{10,11... | collective-permute-start | bytes 393224 | tf_op jit(solution)/shard_map/ppermute | solution.py:22
  61.8 1.0 %fusion.26 = (f32[64,4,4,8,8,1]{0,5,4,3,2,1:T(1,128)S(1)}, f32[64,4,4,8,8,1]{0,5,4,3,2,1:T(1,128)S(1)}) fusion(f32[64,4,4,8,8,8]{0,5,4,3,2,1:T(8,128)S(1)} %select_add_fusion), kind=kLoop, calls=%fused_computation.62 | loop fusion | bytes 1048576 | tf_op jit(solution)/shard_map/slice | solution.py:100
  62.8 4.3 %collective-permute-start.1 = (f32[64,1024]{0,1:T(8,128)S(1)}, f32[64,1024]{0,1:T(8,128)S(1)}, u32[]{:S(2)}, u32[]{:S(2)}) collective-permute-start(f32[64,1024]{0,1:T(8,128)S(1)} %bitcast.104), channel_id=1, source_target_pairs={{0,30},{2,0},{4,2},{6,4},{8,6},{10,8},{12,10},{14,12},{16,14},{18,... | collective-permute-start | bytes 786440 | tf_op jit(solution)/shard_map/ppermute | solution.py:16
  67.3 0.9 and_select_fusion.1
  68.1 0.2 copy.22
  68.3 5.1 %slice.88 = f32[64,4,4,8,8,6]{0,5,4,3,2,1:T(8,128)} slice(f32[64,4,4,8,8,8]{0,5,4,3,2,1:T(8,128)} %copy-done.2), slice={[0:64], [0:4], [0:4], [0:8], [0:8], [1:7]} | slice | bytes 3145728 | tf_op jit(solution)/shard_map/slice | solution.py:108
  73.5 0.2 copy.20
  73.7 0.2 copy.21
  74.0 0.1 broadcast_in_dim.155
  74.3 0.1 broadcast_in_dim.179
  74.5 0.9 fusion.14
  75.4 0.7 collective-permute-start.4
  76.2 1.6 %collective-permute-done.4 = f32[2,64,32]{1,2,0:T(8,128)S(1)} collective-permute-done((f32[2,64,32]{1,2,0:T(8,128)S(1)}, f32[2,64,32]{1,2,0:T(8,128)S(1)}, u32[]{:S(2)}, u32[]{:S(2)}) %collective-permute-start.4) | collective-permute-done | bytes 16416 | tf_op jit(solution)/shard_map/ppermute | solution.py:16
  77.7 0.2 convolution_bitcast_fusion
  78.1 0.5 fusion.10
  78.5 0.2 copy.24
  78.8 0.2 copy.25
  79.2 4.9 %collective-permute-done.3 = f32[2,64,32]{1,2,0:T(8,128)S(1)} collective-permute-done((f32[2,64,32]{1,2,0:T(8,128)S(1)}, f32[2,64,32]{1,2,0:T(8,128)S(1)}, u32[]{:S(2)}, u32[]{:S(2)}) %collective-permute-start.3) | collective-permute-done | bytes 16416 | tf_op jit(solution)/shard_map/ppermute | solution.py:16
  84.1 0.2 fusion.13
  84.4 0.2 copy.27
  84.6 3.0 %collective-permute-done = f32[64,1024]{1,0:T(8,128)S(1)} collective-permute-done((f32[64,1024]{1,0:T(8,128)S(1)}, f32[64,1024]{1,0:T(8,128)S(1)}, u32[]{:S(2)}, u32[]{:S(2)}) %collective-permute-start) | collective-permute-done | bytes 262176 | tf_op jit(solution)/shard_map/ppermute | solution.py:16
  87.7 0.3 convolution_add_fusion
  88.0 0.2 copy.23
  88.2 3.8 %pad_maximum_fusion = f32[64,4,4,8,8,8]{0,5,4,3,2,1:T(8,128)S(1)} fusion(f32[64,4,4,8,8,1]{0,5,4,3,2,1:T(1,128)S(1)} %bitcast.99, f32[64,4,4,8,8,6]{0,5,4,3,2,1:T(8,128)} %slice.88, f32[64,4,4,8,8,1]{0,5,4,3,2,1:T(1,128)S(1)} %bitcast.100), kind=kLoop, calls=%fused_computation.3 | loop fusion | flops 1048576 | bytes 4194304 | tf_op jit(solution)/shard_map/concatenate | solution.py:105
  92.4 2.8 %select_select_fusion = f32[1,64,4,4,512]{1,4,3,2,0:T(8,128)} fusion(f32[1,64,4,4,512]{1,4,3,2,0:T(8,128)S(1)} %bitcast.94, f32[64,4,512]{0,2,1:T(8,128)S(1)} %bitcast.98, f32[64,4,512]{0,2,1:T(8,128)S(1)} %bitcast.97, pred[4,512]{1,0:T(4,128)(4,1)S(1)} %broadcast_in_dim.179, pred[4,512]{1,0:T(4,128)(4,1)S(1)} %broadcast_in_dim.155), kind=kLoop, calls=%fused_computation.4 | loop fusion | flops 1048576 | bytes 5246976 | tf_op jit(solution)/shard_map/jit(_where)/select_n | solution.py:189
  95.1 4.8 %copy.34 = f32[1,64,4,4,512]{4,3,2,1,0:T(4,128)} copy(f32[1,64,4,4,512]{1,4,3,2,0:T(8,128)} %select_select_fusion) | data formatting | bytes 4194304 | tf_op jit(solution)/shard_map/jit(_where)/select_n | solution.py:189
  (45 shorter events, 1.7 us)
Async XLA Ops:
  0.0 20.8 %copy-start = (f32[1,64,4,4,512]{4,3,2,1,0:T(4,128)S(1)}, f32[1,64,4,4,512]{4,3,2,1,0:T(4,128)}, u32[]{:S(2)}) copy-start(f32[1,64,4,4,512]{4,3,2,1,0:T(4,128)} %param.6) | copy-start | bytes 6291460
  20.8 13.6 %copy-start.3 = (f32[64,4,4,1536]{3,0,2,1:T(8,128)S(1)}, f32[64,4,4,1536]{3,0,2,1:T(8,128)}, u32[]{:S(2)}) copy-start(f32[64,4,4,1536]{3,0,2,1:T(8,128)} %reshape.145) | copy-start | bytes 18874372
  20.8 13.6 %copy-start.4 = (f32[1536,512,1,1]{1,0,3,2:T(8,128)S(1)}, f32[1536,512,1,1]{1,0,3,2:T(8,128)}, u32[]{:S(2)}) copy-start(f32[1536,512,1,1]{1,0,3,2:T(8,128)} %constant.85) | copy-start | bytes 9437188
  20.8 13.6 %copy-start.5 = (f32[1536]{0:T(1024)S(1)}, f32[1536]{0:T(1024)}, u32[]{:S(2)}) copy-start(f32[1536]{0:T(1024)} %constant.74.clone) | copy-start | bytes 18436
  58.6 3.1 %copy-start.2 = (f32[64,4,4,8,8,8]{0,5,4,3,2,1:T(8,128)}, f32[64,4,4,8,8,8]{0,5,4,3,2,1:T(8,128)S(1)}, u32[]{:S(2)}) copy-start(f32[64,4,4,8,8,8]{0,5,4,3,2,1:T(8,128)S(1)} %select_add_fusion) | copy-start | bytes 6291460
  58.7 16.7 %collective-permute-start.2 = (f32[2,64,256]{1,2,0:T(8,128)S(1)}, f32[2,64,256]{1,2,0:T(8,128)S(1)}, u32[]{:S(2)}, u32[]{:S(2)}) collective-permute-start(f32[2,64,256]{1,2,0:T(8,128)S(1)} %pad_maximum_fusion.1), channel_id=1, source_target_pairs={{0,1},{1,0},{2,3},{3,2},{4,5},{5,4},{6,7},{7,6},{8,9},{9,8},{10,11... | collective-permute-start | bytes 393224 | tf_op jit(solution)/shard_map/ppermute | solution.py:22
  62.8 15.3 %collective-permute-start.1 = (f32[64,1024]{0,1:T(8,128)S(1)}, f32[64,1024]{0,1:T(8,128)S(1)}, u32[]{:S(2)}, u32[]{:S(2)}) collective-permute-start(f32[64,1024]{0,1:T(8,128)S(1)} %bitcast.104), channel_id=1, source_target_pairs={{0,30},{2,0},{4,2},{6,4},{8,6},{10,8},{12,10},{14,12},{16,14},{18,... | collective-permute-start | bytes 786440 | tf_op jit(solution)/shard_map/ppermute | solution.py:16
  75.4 2.3 %collective-permute-start.4 = (f32[2,64,32]{1,2,0:T(8,128)S(1)}, f32[2,64,32]{1,2,0:T(8,128)S(1)}, u32[]{:S(2)}, u32[]{:S(2)}) collective-permute-start(f32[2,64,32]{1,2,0:T(8,128)S(1)} %bitcast.115), channel_id=1, source_target_pairs={{0,30},{2,0},{4,2},{6,4},{8,6},{10,8},{12,10},{14,12},{16,14},{18,... | collective-permute-start | bytes 49160 | tf_op jit(solution)/shard_map/ppermute | solution.py:16
  78.0 6.1 %collective-permute-start.3 = (f32[2,64,32]{1,2,0:T(8,128)S(1)}, f32[2,64,32]{1,2,0:T(8,128)S(1)}, u32[]{:S(2)}, u32[]{:S(2)}) collective-permute-start(f32[2,64,32]{1,2,0:T(8,128)S(1)} %get-tuple-element.23), channel_id=1, source_target_pairs={{0,2},{2,4},{4,6},{6,8},{8,10},{10,12},{12,14},{14,16},{16,18},{18... | collective-permute-start | bytes 49160 | tf_op jit(solution)/shard_map/ppermute | solution.py:16
  79.1 8.5 %collective-permute-start = (f32[64,1024]{1,0:T(8,128)S(1)}, f32[64,1024]{1,0:T(8,128)S(1)}, u32[]{:S(2)}, u32[]{:S(2)}) collective-permute-start(f32[64,1024]{1,0:T(8,128)S(1)} %get-tuple-element.13), channel_id=1, source_target_pairs={{0,2},{2,4},{4,6},{6,8},{8,10},{10,12},{12,14},{14,16},{16,18},{18... | collective-permute-start | bytes 786440 | tf_op jit(solution)/shard_map/ppermute | solution.py:16
  92.3 7.6 %copy-start.1 = (f32[1,64,4,4,512]{4,3,2,1,0:T(4,128)S(1)}, f32[1,64,4,4,512]{4,3,2,1,0:T(4,128)}, u32[]{:S(2)}) copy-start(f32[1,64,4,4,512]{4,3,2,1,0:T(4,128)} %param.6) | copy-start | bytes 6291460
where the time goes:
time: 101 us; the launch traced here: 100 us
  matrix products  35.7 us (35%)
  local copies, waits for them, and re-layouts  34.4 us (34%)
  other arithmetic  11.7 us (12%)
  waiting for transfers between devices  9.51 us (9%)
  starting transfers between devices  8.23 us (8%)
    dot_general x1, matrix products, local_apply(): jnp.dot(fluxes, operator_stack, precision=highest, preferred_element_type...  21 us
    dot_general x1, matrix products, local_apply(): jnp.dot(values, operator_stack.T, precision=highest, preferred_element_ty...  13.5 us
    reshape x1, local copies, waits for them, and re-layouts, body(): factors = metric.reshape(slab_count, EZ, EY, 3 * PTS)  11.4 us
    ppermute x4, waiting for transfers between devices, from_behind(): lax.ppermute(array, axis, [(i, (i + by) % peers) for i in range(peers)])  9.51 us
    unnamed x13, local copies, waits for them, and re-layouts  9.43 us
    ppermute x4, starting transfers between devices, from_behind(): lax.ppermute(array, axis, [(i, (i + by) % peers) for i in range(peers)])  5.17 us
    slice x1, local copies, waits for them, and re-layouts, put_faces(): local_out[..., 1:P_SIZE - 1]  5.13 us
    select_n x1, local copies, waits for them, and re-layouts, body(): local_out = jnp.where(top_mask, top_grid, local_out)  4.8 us
  transfers between devices with their start and end apart: 5, of which 3 were waited for; matrix products, arithmetic and copies ran while one was open for 11% of the time, Pallas kernels for 0%

commit v1 on v0

v1 whole, which is shorter than its diff:
```python
import jax
import jax.numpy as jnp
import numpy as np
from jax import lax
from jax.experimental import pallas as pl
from jax.experimental.pallas import tpu as pltpu
from jax.sharding import PartitionSpec as P

P_SIZE = 8
PTS = 512
EY = 4
EZ = 4
TILES = EZ * 2
BLOCK = 8
FIX_BLOCK = 8


def legendre_pair(gll_nodes, degree):
    lower_poly = gll_nodes * 0.0 + 1.0
    upper_poly = gll_nodes.copy()
    for poly_order in range(2, degree + 1):
        lower_poly, upper_poly = (
            upper_poly,
            ((2 * poly_order - 1) * gll_nodes * upper_poly - (poly_order - 1) * lower_poly)
            / poly_order,
        )
    return (lower_poly, upper_poly)


def gll_tables():
    degree = P_SIZE - 1
    gll_nodes = -np.cos(np.pi * np.arange(P_SIZE) / degree)
    for newton_sweep in range(100):
        lower_poly, upper_poly = legendre_pair(gll_nodes, degree)
        gll_nodes = gll_nodes - (gll_nodes * upper_poly - lower_poly) / ((degree + 1) * upper_poly)
    lower_poly, upper_poly = legendre_pair(gll_nodes, degree)
    quad_weights = 2.0 / (degree * (degree + 1) * upper_poly * upper_poly)
    identity = np.eye(P_SIZE)
    differ = gll_nodes[:, None] - gll_nodes[None, :] + identity
    derivative = upper_poly[:, None] / (upper_poly[None, :] * differ)
    derivative = derivative * (1.0 - identity)
    derivative[0, 0] = -degree * (degree + 1) / 4.0
    derivative[degree, degree] = degree * (degree + 1) / 4.0
    return derivative, quad_weights


def split_table(table):
    high = table.astype(np.float32).astype(jnp.bfloat16)
    low = (table - high.astype(np.float64)).astype(np.float32).astype(jnp.bfloat16)
    return high, low


def kernel_tables():
    derivative, rho = gll_tables()
    two = np.eye(2)
    eye = np.eye(P_SIZE)
    plane = np.tile(np.kron(rho, rho), 2)
    along_x = np.kron(two, np.kron(eye, derivative))
    along_y = np.kron(two, np.kron(derivative, eye))
    forward = np.concatenate([along_x.T * plane[None, :], along_y.T * plane[None, :]], 1)
    backward = np.concatenate([along_x, along_y], 0)
    f_high, f_low = split_table(forward)
    b_high, b_low = split_table(backward)
    fwd_a = np.concatenate([f_high, f_high], 0)
    bwd_a = np.concatenate([b_high, b_low], 1)
    sub = np.arange(8)[:, None]
    lane = np.arange(128)[None, :]
    point = lane % 64
    in_plane = rho[point // 8] * rho[point % 8]
    z_fwd = np.zeros((2, 8, 8, 128))
    z_bwd = np.zeros((2, 8, 8, 128))
    rho_c = np.zeros((2, 8, 128))
    for half in range(2):
        c = 4 * half + 2 * (sub // 4) + lane // 64
        rho_c[half] = rho[c]
        for source in range(2):
            for swap_sub in range(2):
                for swap_lane in range(2):
                    other = 4 * source + 2 * (sub // 4 ^ swap_sub) + (lane // 64 ^ swap_lane)
                    k = source * 4 + swap_sub * 2 + swap_lane
                    z_fwd[half, k] = derivative[c, other] * rho[c] * in_plane
                    z_bwd[half, k] = derivative[other, c]
    coeffs = np.concatenate(
        [z_fwd.reshape(16, 8, 128), z_bwd.reshape(16, 8, 128), rho_c], 0
    )
    tables = (fwd_a, f_low, bwd_a, b_high, coeffs.astype(np.float32))
    return tuple(jnp.asarray(table) for table in tables)


def split(value):
    high = value.astype(jnp.bfloat16)
    low = (value - high.astype(jnp.float32)).astype(jnp.bfloat16)
    return high, low


def dot(a, b):
    return jnp.dot(a, b, preferred_element_type=jnp.float32)


def along_z(pair, coeffs, base):
    variants = []
    for value in pair:
        turned = pltpu.roll(value, 64, 1)
        variants += [value, turned, pltpu.roll(value, 4, 0), pltpu.roll(turned, 4, 0)]
    out = []
    for half in range(2):
        terms = [coeffs[base + half * 8 + k] * variants[k] for k in range(8)]
        while len(terms) > 1:
            terms = [terms[i] + terms[i + 1] for i in range(0, len(terms), 2)]
        out.append(terms[0])
    return out


def lanes_from(value, index):
    return jnp.take_along_axis(value, index, axis=1, mode="promise_in_bounds")


def flip(value, sub, lane):
    value = lanes_from(value, lane ^ 7)
    odd = jnp.where(sub % 2 == 0, pltpu.roll(value, 7, 0), pltpu.roll(value, 1, 0))
    return jnp.where(sub % 4 < 2, pltpu.roll(odd, 6, 0), pltpu.roll(odd, 2, 0))


def iotas():
    sub = lax.broadcasted_iota(jnp.int32, (8, 128), 0)
    lane = lax.broadcasted_iota(jnp.int32, (8, 128), 1)
    return sub, lane


def turned_flag(map_ref, row):
    return jnp.broadcast_to(map_ref[pl.ds(row, 1), 0:1], (8, 128)) != 0


def apply_kernel(
    u_ref, m_ref, map_ref, fa_ref, fl_ref, ba_ref, bh_ref, co_ref,
    out_ref, left_ref, right_ref, zed_ref, el_ref, er_ref,
    g_ref, fh_ref, fl2_ref, lz_ref, l_ref,
):
    step = pl.program_id(0)
    sub, lane = iotas()
    rows = u_ref.shape[0]
    slabs = rows // 64
    u = u_ref[...].reshape(slabs * EZ, 2, 8, 128)
    v = (u * co_ref[32:34][None]).reshape(rows, 128)
    high, low = split(v)
    uk = jnp.concatenate([high, low], 1)
    g_ref[...] = dot(uk, fa_ref[...]) + dot(high, fl_ref[...])

    for e in range(slabs * EZ):
        base = e * 16
        mbase = e * 48
        pair = [u_ref[base : base + 8, :], u_ref[base + 8 : base + 16, :]]
        grad = along_z(pair, co_ref, 0)
        flux = [
            grad[h] * m_ref[mbase + 32 + 8 * h : mbase + 40 + 8 * h, :] for h in range(2)
        ]
        back = along_z(flux, co_ref, 16)
        for h in range(2):
            lz_ref[base + 8 * h : base + 8 * h + 8, :] = back[h]
        fx = m_ref[mbase : mbase + 16, :] * g_ref[base : base + 16, :128]
        fy = m_ref[mbase + 16 : mbase + 32, :] * g_ref[base : base + 16, 128:]
        xh, xl = split(fx)
        yh, yl = split(fy)
        fh_ref[base : base + 16, :128] = xh
        fh_ref[base : base + 16, 128:] = yh
        fl2_ref[base : base + 16, :128] = xl
        fl2_ref[base : base + 16, 128:] = yl
    both = dot(fh_ref[...], ba_ref[...])
    l_ref[...] = both[:, :128] + both[:, 128:] + dot(fl2_ref[...], bh_ref[...]) + lz_ref[...]

    b = lane // 8 % 8
    ey = sub % 4
    after_mask = (b == 7) & (ey < 3)
    before_mask = (b == 0) & (ey > 0)
    high_c = (sub >= 4) & (lane >= 64)
    low_c = (sub < 4) & (lane < 64)
    index_left = lane % 16 * 8
    index_right = index_left + 7
    slot = lane // 16
    slot8 = lane // 8
    for s in range(slabs):
        tiles = []
        for k in range(TILES):
            row = s * 64 + k * 8
            t = l_ref[row : row + 8, :]
            after = pltpu.roll(pltpu.roll(t, 56, 1), 7, 0)
            before = pltpu.roll(pltpu.roll(t, 72, 1), 1, 0)
            tiles.append(
                t + jnp.where(after_mask, after, 0.0) + jnp.where(before_mask, before, 0.0)
            )
        for e in range(EZ - 1):
            top = tiles[2 * e + 1]
            bottom = tiles[2 * e + 2]
            tiles[2 * e + 1] = top + jnp.where(
                high_c, pltpu.roll(pltpu.roll(bottom, 64, 1), 4, 0), 0.0
            )
            tiles[2 * e + 2] = bottom + jnp.where(
                low_c, pltpu.roll(pltpu.roll(top, 64, 1), 4, 0), 0.0
            )
        left = jnp.zeros((8, 128), jnp.float32)
        right = left
        for k in range(TILES):
            row = s * 64 + k * 8
            out_ref[row : row + 8, :] = tiles[k]
            left = jnp.where(slot == k, lanes_from(tiles[k], index_left), left)
            right = jnp.where(slot == k, lanes_from(tiles[k], index_right), right)
        flag = turned_flag(map_ref, step * slabs + s)
        right = jnp.where(flag, flip(right, sub, lane), right)
        left_ref[s * 8 : s * 8 + 8, :] = left
        right_ref[s * 8 : s * 8 + 8, :] = right
        zed = jnp.where(sub < 4, tiles[0], tiles[TILES - 1])
        if s % 2 == 0:
            even = zed
        else:
            odd = pltpu.roll(zed, 64, 1)
            zed_ref[s // 2 * 8 : s // 2 * 8 + 8, :] = jnp.where(
                (sub < 4) == (lane < 64), even, odd
            )
        place = step * slabs + s
        place16 = place % 16
        mask = ((slot8 == place16) & (sub < 4)) | (
            (slot8 == (place16 + 15) % 16) & (sub >= 4)
        )
        if s == 0:
            acc_l = jnp.zeros((8, 128), jnp.float32)
            acc_r = acc_l
        acc_l = jnp.where(mask, pltpu.roll(left, place16 * 8, 1), acc_l)
        acc_r = jnp.where(mask, pltpu.roll(right, place16 * 8, 1), acc_r)
    per = 16 // slabs
    first = step % per == 0
    where = pl.ds(pl.multiple_of(step // per * 8, 8), 8)
    el_ref[where, :] = jnp.where(first, acc_l, el_ref[where, :] + acc_l)
    er_ref[where, :] = jnp.where(first, acc_r, er_ref[where, :] + acc_r)


def fix_kernel(
    prev_ref, next_ref, in_ref, map_ref, fprev_ref, fnext_ref, zed_ref, eprev_ref, enext_ref,
    out_ref,
):
    step = pl.program_id(0)
    sub, lane = iotas()
    slabs = in_ref.shape[0] // 64
    a = lane % 8
    low_c = (sub < 4) & (lane < 64)
    high_c = (sub >= 4) & (lane >= 64)
    low_edge = (sub < 4) & (lane < 8)
    high_edge = (sub >= 4) & (lane >= 120)

    def incoming(face_ref, edge_ref, j):
        face = face_ref[pl.ds(pl.multiple_of(j * 8, 8), 8), :]
        edge = edge_ref[pl.ds(pl.multiple_of(j // 16 * 8, 8), 8), :]
        shift = (16 - j % 16) % 16 * 8
        edge = pltpu.roll(pltpu.roll(edge, shift, 1), 4, 0)
        edge = jnp.where(
            low_edge,
            pltpu.roll(edge, 8, 1),
            jnp.where(high_edge, pltpu.roll(edge, 120, 1), 0.0),
        )
        return face + edge

    for s in range(slabs):
        p = step * slabs + s
        left = incoming(fprev_ref, eprev_ref, prev_ref[p])
        right = incoming(fnext_ref, enext_ref, next_ref[p])
        right = jnp.where(turned_flag(map_ref, p), flip(right, sub, lane), right)
        zed = pltpu.roll(zed_ref[s // 2 * 8 : s // 2 * 8 + 8, :], 4, 0)
        if s % 2 == 0:
            zed = pltpu.roll(zed, 64, 1)
        for k in range(TILES):
            row = s * 64 + k * 8
            index = k * 16 + lane // 8
            t = in_ref[row : row + 8, :]
            t = t + jnp.where(a == 0, lanes_from(left, index), 0.0)
            t = t + jnp.where(a == 7, lanes_from(right, index), 0.0)
            if k == 0:
                t = t + jnp.where(low_c, zed, 0.0)
            if k == TILES - 1:
                t = t + jnp.where(high_c, zed, 0.0)
            out_ref[row : row + 8, :] = t


def whole_of(array):
    return pl.BlockSpec(array.shape, lambda i, *_: (0,) * array.ndim)


def apply_local(u, m, face_map, tables, slab_count):
    steps = slab_count // BLOCK
    rows = BLOCK * 64
    f32 = jnp.float32
    shapes = [
        (slab_count * 64, 128),
        (slab_count * 8, 128),
        (slab_count * 8, 128),
        (slab_count * 4, 128),
        (slab_count // 2, 128),
        (slab_count // 2, 128),
    ]
    row_block = lambda n: pl.BlockSpec((n, 128), lambda i: (i, 0))
    return pl.pallas_call(
        apply_kernel,
        grid=(steps,),
        in_specs=[
            row_block(rows),
            row_block(rows * 3),
            pl.BlockSpec((slab_count, 128), lambda i: (0, 0)),
        ]
        + [whole_of(t) for t in tables],
        out_specs=[
            row_block(rows),
            row_block(BLOCK * 8),
            row_block(BLOCK * 8),
            row_block(BLOCK * 4),
            pl.BlockSpec(shapes[4], lambda i: (0, 0)),
            pl.BlockSpec(shapes[5], lambda i: (0, 0)),
        ],
        out_shape=[jax.ShapeDtypeStruct(s, f32) for s in shapes],
        scratch_shapes=[
            pltpu.VMEM((rows, 256), f32),
            pltpu.VMEM((rows, 256), jnp.bfloat16),
            pltpu.VMEM((rows, 256), jnp.bfloat16),
            pltpu.VMEM((rows, 128), f32),
            pltpu.VMEM((rows, 128), f32),
        ],
        name="apply_local",
    )(u, m, face_map, *tables)


def fix_faces(prev_index, next_index, local, face_map, fprev, fnext, zed, eprev, enext):
    slab_count = face_map.shape[0]
    steps = slab_count // FIX_BLOCK
    rows = FIX_BLOCK * 64
    return pl.pallas_call(
        fix_kernel,
        grid_spec=pltpu.PrefetchScalarGridSpec(
            num_scalar_prefetch=2,
            grid=(steps,),
            in_specs=[
                pl.BlockSpec((rows, 128), lambda i, *_: (i, 0)),
                pl.BlockSpec((slab_count, 128), lambda i, *_: (0, 0)),
                whole_of(fprev),
                whole_of(fnext),
                pl.BlockSpec((FIX_BLOCK * 4, 128), lambda i, *_: (i, 0)),
                whole_of(eprev),
                whole_of(enext),
            ],
            out_specs=pl.BlockSpec((rows, 128), lambda i, *_: (i, 0)),
        ),
        out_shape=jax.ShapeDtypeStruct(local.shape, jnp.float32),
        name="fix_faces",
    )(prev_index, next_index, local, face_map, fprev, fnext, zed, eprev, enext)


def send(value, by, across):
    slabs = lax.axis_size("slab")
    layers = lax.axis_size("layer")
    pairs = [
        (s * layers + l, (s + by) % slabs * layers + (l + across) % layers)
        for s in range(slabs)
        for l in range(layers)
    ]
    return lax.ppermute(value, ("slab", "layer"), pairs)


def body(nodal_field, metric, slab_ids, face_map):
    slab_count = nodal_field.shape[1]
    cycle_size = lax.axis_size("slab")
    total_slabs = slab_count * cycle_size
    device = lax.axis_index("slab")
    u = nodal_field.reshape(slab_count, EZ, EY, 4, 128).transpose(0, 1, 3, 2, 4)
    u = u.reshape(slab_count * 64, 128)
    m = metric.reshape(slab_count, EZ, EY, 3, 4, 128).transpose(0, 1, 3, 4, 2, 5)
    m = m.reshape(slab_count * 192, 128)
    local, left, right, zed, edge_left, edge_right = apply_local(
        u, m, face_map, kernel_tables(), slab_count
    )
    zed = send(zed, 0, 1)
    fprev = send(right, 1, 0)
    fnext = send(left, -1, 0)
    eprev = send(edge_right, 1, 1)
    enext = send(edge_left, -1, 1)

    def ids_of(index):
        return lax.dynamic_slice_in_dim(slab_ids, index % cycle_size * slab_count, slab_count)

    own_ids = ids_of(device)
    position = jnp.arange(slab_count, dtype=jnp.int32)[None, :]

    def index_of(there, wanted):
        hit = there[None, :] == wanted[:, None]
        return jnp.sum(jnp.where(hit, position, 0), axis=1)

    prev_index = index_of(
        ids_of(device + cycle_size - 1), (own_ids + total_slabs - 1) % total_slabs
    )
    next_index = index_of(ids_of(device + 1), (own_ids + 1) % total_slabs)
    out = fix_faces(prev_index, next_index, local, face_map, fprev, fnext, zed, eprev, enext)
    out = out.reshape(slab_count, EZ, 4, EY, 128).transpose(0, 1, 3, 2, 4)
    return out.reshape(1, slab_count, EZ, EY, PTS)


def solution(mesh):
    return jax.shard_map(
        body,
        mesh=mesh,
        in_specs=(
            P("layer", "slab", None, None, None),
            P("layer", "slab", None, None, None, None),
            P(),
            P("slab", None),
        ),
        out_specs=P("layer", "slab", None, None, None),
        check_vma=False,
    )
```

time: 101 us -> 43.1 us (0.43)
  matrix products: 35.7 us -> 0 us
  local copies, waits for them, and re-layouts: 34.4 us -> 0.82 us
  Pallas kernels: 0 us -> 25.8 us
  other arithmetic: 11.7 us -> 1.63 us
  waiting for transfers between devices: 9.51 us -> 1.62 us
  starting transfers between devices: 8.23 us -> 12.8 us
    dot_general x6 -> x0, matrix products: 35.7 us -> none  [the longest x1 21 us: local_apply(): jnp.dot(fluxes, operator_stack, precision=highest, preferred_element_type...]
    pallas_call x0 -> x2, Pallas kernels: none -> 25.8 us  [the longest x1 16.6 us: apply_local(): pl.pallas_call(apply_kernel, grid=(steps,), in_specs=[row_block(rows), ro...]
    reshape x3 -> x0, local copies, waits for them, and re-layouts: 11.8 us -> none  [the longest x1 11.4 us: body(): factors = metric.reshape(slab_count, EZ, EY, 3 * PTS)]
    unnamed x13 -> x10, local copies, waits for them, and re-layouts: 9.43 us -> 0.82 us
    ppermute x5, waiting for transfers between devices: 9.51 us -> 1.62 us  [send(): return lax.ppermute(value, ('slab', 'layer'), pairs)]
    slice x7 -> x0, local copies, waits for them, and re-layouts: 6.36 us -> none  [the longest x1 5.13 us: put_faces(): local_out[..., 1:P_SIZE - 1]]
    select_n x1 -> x0, local copies, waits for them, and re-layouts: 4.8 us -> none  [body(): local_out = jnp.where(top_mask, top_grid, local_out)]
    ppermute x5, starting transfers between devices: 8.23 us -> 12.8 us  [send(): return lax.ppermute(value, ('slab', 'layer'), pairs)]
  transfers between devices with their start and end apart: 5 -> 5, of which waited for: 3 -> 1; matrix products, arithmetic and copies ran while one was open for 11% -> 4% of each run, Pallas kernels for 0% -> 0%
where the time goes in v1:
time: 43.1 us; the launch traced here: 42.8 us
  Pallas kernels  25.8 us (60%)
  starting transfers between devices  12.8 us (30%)
  other arithmetic  1.63 us (4%)
  waiting for transfers between devices  1.62 us (4%)
  local copies, waits for them, and re-layouts  0.82 us (2%)
    pallas_call x1, Pallas kernels, apply_local(): pl.pallas_call(apply_kernel, grid=(steps,), in_specs=[row_block(rows), ro...  16.6 us
    ppermute x5, starting transfers between devices, send(): return lax.ppermute(value, ('slab', 'layer'), pairs)  12.8 us
    pallas_call x1, Pallas kernels, fix_faces(): pl.pallas_call(fix_kernel, grid_spec=pltpu.PrefetchScalarGridSpec(num_sca...  9.23 us
    ppermute x5, waiting for transfers between devices, send(): return lax.ppermute(value, ('slab', 'layer'), pairs)  1.62 us
    select_n x1, other arithmetic, body(): next_index = index_of(ids_of(device + 1), (own_ids + 1) % total_slabs)  0.88 us
  transfers between devices with their start and end apart: 5, of which 1 were waited for; matrix products, arithmetic and copies ran while one was open for 4% of the time, Pallas kernels for 0%

profile of v1, /device:TPU:0, one launch (start us, length us, event | category | flops | bytes accessed | tf_op | source)
XLA Modules:
  0.0 42.8 jit_solution(8966284282410637279)
XLA Ops:
  0.0 16.6 %apply_local.1 = (f32[4096,128]{1,0:T(8,128)}, f32[512,128]{1,0:T(8,128)}, f32[512,128]{1,0:T(8,128)}, f32[256,128]{1,0:T(8,128)}, f32[32,128]{1,0:T(8,128)}, /*index=5*/f32[32,128]{1,0:T(8,128)}) custom-call(f32[4096,128]{1,0:T(8,128)} %bitcast.16, f32[12288,128]{1,0:T(8,128)} %bitcast.15, s32[64,1024]{1,0:T(8,128)} %map_ref.3, ...), custom_call_target="tpu_custom_call" | custom-call | tf_op jit(solution)/shard_map/apply_local/pallas_call | solution.py:299
  16.6 0.5 %collective-permute-start = (f32[512,128]{1,0:T(8,128)}, f32[512,128]{1,0:T(8,128)S(1)}, u32[]{:S(2)}, u32[]{:S(2)}) collective-permute-start(f32[512,128]{1,0:T(8,128)} %get-tuple-element.12), channel_id=1, source_target_pairs={{0,2},{1,3},{2,4},{3,5},{4,6},{5,7},{6,8},{7,9},{8,10},{9,11},{10,... | collective-permute-start | bytes 786440 | tf_op jit(solution)/shard_map/ppermute | solution.py:361
  17.1 5.0 %collective-permute-start.1 = (f32[512,128]{1,0:T(8,128)}, f32[512,128]{1,0:T(8,128)S(1)}, u32[]{:S(2)}, u32[]{:S(2)}) collective-permute-start(f32[512,128]{1,0:T(8,128)} %get-tuple-element.13), channel_id=1, source_target_pairs={{0,30},{1,31},{2,0},{3,1},{4,2},{5,3},{6,4},{7,5},{8,6},{9,7},{10,... | collective-permute-start | bytes 786440 | tf_op jit(solution)/shard_map/ppermute | solution.py:361
  22.2 0.0 collective-permute-start.3
  22.2 5.3 %collective-permute-start.4 = (f32[32,128]{1,0:T(8,128)}, f32[32,128]{1,0:T(8,128)S(1)}, u32[]{:S(2)}, u32[]{:S(2)}) collective-permute-start(f32[32,128]{1,0:T(8,128)} %get-tuple-element.16), channel_id=1, source_target_pairs={{0,31},{1,30},{2,1},{3,0},{4,3},{5,2},{6,5},{7,4},{8,7},{9,6},{10,... | collective-permute-start | bytes 49160 | tf_op jit(solution)/shard_map/ppermute | solution.py:361
  27.5 1.9 %collective-permute-start.2 = (f32[256,128]{1,0:T(8,128)}, f32[256,128]{1,0:T(8,128)S(1)}, u32[]{:S(2)}, u32[]{:S(2)}) collective-permute-start(f32[256,128]{1,0:T(8,128)} %get-tuple-element.14), channel_id=1, source_target_pairs={{0,1},{1,0},{2,3},{3,2},{4,5},{5,4},{6,7},{7,6},{8,9},{9,8},{10,11... | collective-permute-start | bytes 393224 | tf_op jit(solution)/shard_map/ppermute | solution.py:361
  29.4 0.9 %and_select_fusion = (s32[64]{0:T(128)S(1)}, s32[64]{0:T(128)S(1)}, s32[64]{0:T(128)S(1)}, s32[64]{0:T(128)S(1)}) fusion(s32[1024]{0:T(1024)} %param.11, s32[]{:T(128)S(6)} %select_n.44, s32[]{:T(128)S(6)} %select_n.42, s32[]{:T(128)S(6)} %select_n.48), kind=kLoop, calls=%fused_computation.6 | loop fusion | flops 1536 | bytes 1804 | tf_op jit(solution)/shard_map/jit(remainder)/select_n | solution.py:395
  30.3 0.8 %select_reduce_fusion = (s32[64]{0:T(128)}, s32[64]{0:T(128)}) fusion(s32[64]{0:T(128)S(1)} %get-tuple-element.19, s32[64]{0:T(128)S(1)} %get-tuple-element.17, s32[64]{0:T(128)S(1)} %get-tuple-element.20, s32[64]{0:T(128)S(1)} %get-tuple-element.18), kind=kLoop, calls=%fused_computation | loop fusion | flops 24448 | bytes 1536 | tf_op jit(solution)/shard_map/reduce_sum | solution.py:390
  31.1 0.0 collective-permute-done.3.eprev_ref
  31.1 0.0 copy-start.3
  31.1 0.0 collective-permute-done.4.enext_ref
  31.1 0.0 copy-start.4
  31.1 1.6 %collective-permute-done.2.zed_ref = f32[256,128]{1,0:T(8,128)S(1)} collective-permute-done((f32[256,128]{1,0:T(8,128)}, f32[256,128]{1,0:T(8,128)S(1)}, u32[]{:S(2)}, u32[]{:S(2)}) %collective-permute-start.2) | collective-permute-done | bytes 131104 | tf_op jit(solution)/shard_map/ppermute | solution.py:361
  32.7 0.0 copy-start.2
  32.7 0.0 collective-permute-done.fprev_ref
  32.7 0.0 copy-start
  32.7 0.0 collective-permute-done.1.fnext_ref
  32.7 0.0 copy-start.1
  32.7 0.0 copy-done.3
  32.7 0.0 copy-done.4
  32.7 0.6 %copy-done.2 = f32[256,128]{1,0:T(8,128)} copy-done((f32[256,128]{1,0:T(8,128)}, f32[256,128]{1,0:T(8,128)S(1)}, u32[]{:S(2)}) %copy-start.2) | copy-done | bytes 131096
  33.3 0.1 copy-done
  33.4 0.1 copy-done.1
  33.5 9.2 %fix_faces.1 = f32[4096,128]{1,0:T(8,128)} custom-call(s32[64]{0:T(128)} %get-tuple-element.22.prev_ref, s32[64]{0:T(128)} %get-tuple-element.21.next_ref, f32[4096,128]{1,0:T(8,128)} %get-tuple-element.11.in_ref, s32[64,1024]{1,0:T(8,128)} %map_ref.3, f32[512,128]{1,0:T(8,128)} %copy-done, f32[512,128]{1,0:T(8,128)} %copy-done.1, f32[256,128]{1,0:T(8,128)} %copy-done.2, ...), custom_call_target="tpu_custom_call" | custom-call | tf_op jit(solution)/shard_map/fix_faces/pallas_call | solution.py:332
Async XLA Ops:
  16.6 16.1 %collective-permute-start = (f32[512,128]{1,0:T(8,128)}, f32[512,128]{1,0:T(8,128)S(1)}, u32[]{:S(2)}, u32[]{:S(2)}) collective-permute-start(f32[512,128]{1,0:T(8,128)} %get-tuple-element.12), channel_id=1, source_target_pairs={{0,2},{1,3},{2,4},{3,5},{4,6},{5,7},{6,8},{7,9},{8,10},{9,11},{10,... | collective-permute-start | bytes 786440 | tf_op jit(solution)/shard_map/ppermute | solution.py:361
  17.1 15.5 %collective-permute-start.1 = (f32[512,128]{1,0:T(8,128)}, f32[512,128]{1,0:T(8,128)S(1)}, u32[]{:S(2)}, u32[]{:S(2)}) collective-permute-start(f32[512,128]{1,0:T(8,128)} %get-tuple-element.13), channel_id=1, source_target_pairs={{0,30},{1,31},{2,0},{3,1},{4,2},{5,3},{6,4},{7,5},{8,6},{9,7},{10,... | collective-permute-start | bytes 786440 | tf_op jit(solution)/shard_map/ppermute | solution.py:361
  22.2 8.9 %collective-permute-start.3 = (f32[32,128]{1,0:T(8,128)}, f32[32,128]{1,0:T(8,128)S(1)}, u32[]{:S(2)}, u32[]{:S(2)}) collective-permute-start(f32[32,128]{1,0:T(8,128)} %get-tuple-element.15), channel_id=1, source_target_pairs={{0,3},{1,2},{2,5},{3,4},{4,7},{5,6},{6,9},{7,8},{8,11},{9,10},{10,... | collective-permute-start | bytes 49160 | tf_op jit(solution)/shard_map/ppermute | solution.py:361
  22.2 8.9 %collective-permute-start.4 = (f32[32,128]{1,0:T(8,128)}, f32[32,128]{1,0:T(8,128)S(1)}, u32[]{:S(2)}, u32[]{:S(2)}) collective-permute-start(f32[32,128]{1,0:T(8,128)} %get-tuple-element.16), channel_id=1, source_target_pairs={{0,31},{1,30},{2,1},{3,0},{4,3},{5,2},{6,5},{7,4},{8,7},{9,6},{10,... | collective-permute-start | bytes 49160 | tf_op jit(solution)/shard_map/ppermute | solution.py:361
  27.5 5.2 %collective-permute-start.2 = (f32[256,128]{1,0:T(8,128)}, f32[256,128]{1,0:T(8,128)S(1)}, u32[]{:S(2)}, u32[]{:S(2)}) collective-permute-start(f32[256,128]{1,0:T(8,128)} %get-tuple-element.14), channel_id=1, source_target_pairs={{0,1},{1,0},{2,3},{3,2},{4,5},{5,4},{6,7},{7,6},{8,9},{9,8},{10,11... | collective-permute-start | bytes 393224 | tf_op jit(solution)/shard_map/ppermute | solution.py:361
  31.1 1.6 %copy-start.3 = (f32[32,128]{1,0:T(8,128)}, f32[32,128]{1,0:T(8,128)S(1)}, u32[]{:S(2)}) copy-start(f32[32,128]{1,0:T(8,128)S(1)} %collective-permute-done.3.eprev_ref) | copy-start | bytes 49156
  31.1 1.6 %copy-start.4 = (f32[32,128]{1,0:T(8,128)}, f32[32,128]{1,0:T(8,128)S(1)}, u32[]{:S(2)}) copy-start(f32[32,128]{1,0:T(8,128)S(1)} %collective-permute-done.4.enext_ref) | copy-start | bytes 49156
  32.7 0.7 %copy-start.2 = (f32[256,128]{1,0:T(8,128)}, f32[256,128]{1,0:T(8,128)S(1)}, u32[]{:S(2)}) copy-start(f32[256,128]{1,0:T(8,128)S(1)} %collective-permute-done.2.zed_ref) | copy-start | bytes 393220
  32.7 0.7 %copy-start = (f32[512,128]{1,0:T(8,128)}, f32[512,128]{1,0:T(8,128)S(1)}, u32[]{:S(2)}) copy-start(f32[512,128]{1,0:T(8,128)S(1)} %collective-permute-done.fprev_ref) | copy-start | bytes 786436
  32.7 0.8 %copy-start.1 = (f32[512,128]{1,0:T(8,128)}, f32[512,128]{1,0:T(8,128)S(1)}, u32[]{:S(2)}) copy-start(f32[512,128]{1,0:T(8,128)S(1)} %collective-permute-done.1.fnext_ref) | copy-start | bytes 786436

commit v2 on v1

v2 whole, which is shorter than its diff:
```python
import functools

import jax
import jax.numpy as jnp
import numpy as np
from jax import lax
from jax.experimental import pallas as pl
from jax.experimental.pallas import tpu as pltpu
from jax.sharding import PartitionSpec as P

P_SIZE = 8
PTS = 512
EY = 4
EZ = 4
TILES = EZ * 2
BLOCK = 8
FIX_BLOCK = 16


def legendre_pair(gll_nodes, degree):
    lower_poly = gll_nodes * 0.0 + 1.0
    upper_poly = gll_nodes.copy()
    for poly_order in range(2, degree + 1):
        lower_poly, upper_poly = (
            upper_poly,
            ((2 * poly_order - 1) * gll_nodes * upper_poly - (poly_order - 1) * lower_poly)
            / poly_order,
        )
    return (lower_poly, upper_poly)


def gll_tables():
    degree = P_SIZE - 1
    gll_nodes = -np.cos(np.pi * np.arange(P_SIZE) / degree)
    for newton_sweep in range(100):
        lower_poly, upper_poly = legendre_pair(gll_nodes, degree)
        gll_nodes = gll_nodes - (gll_nodes * upper_poly - lower_poly) / ((degree + 1) * upper_poly)
    lower_poly, upper_poly = legendre_pair(gll_nodes, degree)
    quad_weights = 2.0 / (degree * (degree + 1) * upper_poly * upper_poly)
    identity = np.eye(P_SIZE)
    differ = gll_nodes[:, None] - gll_nodes[None, :] + identity
    derivative = upper_poly[:, None] / (upper_poly[None, :] * differ)
    derivative = derivative * (1.0 - identity)
    derivative[0, 0] = -degree * (degree + 1) / 4.0
    derivative[degree, degree] = degree * (degree + 1) / 4.0
    return derivative, quad_weights


def split_table(table):
    high = table.astype(np.float32).astype(jnp.bfloat16)
    low = (table - high.astype(np.float64)).astype(np.float32).astype(jnp.bfloat16)
    return high, low


def kernel_tables():
    derivative, rho = gll_tables()
    two = np.eye(2)
    eye = np.eye(P_SIZE)
    plane = np.tile(np.kron(rho, rho), 2)
    along_x = np.kron(two, np.kron(eye, derivative))
    along_y = np.kron(two, np.kron(derivative, eye))
    forward = np.concatenate([along_x.T * plane[None, :], along_y.T * plane[None, :]], 1)
    backward = np.concatenate([along_x, along_y], 0)
    f_high, f_low = split_table(forward)
    b_high, b_low = split_table(backward)
    fwd_a = np.concatenate([f_high, f_high], 0)
    bwd_a = np.concatenate([b_high, b_low], 1)
    sub = np.arange(8)[:, None]
    lane = np.arange(128)[None, :]
    point = lane % 64
    in_plane = rho[point // 8] * rho[point % 8]
    rho_c = np.zeros((2, 8, 128))
    for half in range(2):
        rho_c[half] = rho[4 * half + 2 * (sub // 4) + lane // 64]
    c = 2 * (sub // 4) + lane // 64
    parts = []
    for operator, scale in ((derivative, rho_c[0] * in_plane), (derivative.T, 1.0)):
        for sign in (1, -1):
            for swap in range(4):
                near = operator[c, c ^ swap]
                far = operator[c, 7 - (c ^ swap)]
                parts.append((near + sign * far) * 0.5 * scale)
    coeffs = np.concatenate([np.stack(parts), rho_c], 0)
    lane_in = np.arange(128)[:, None]
    lane_out = np.arange(128)[None, :]
    sides = [lane_in == lane_out % 16 * 8 + edge for edge in (0, 7)]
    pick = np.concatenate(sides, 1).astype(jnp.bfloat16)
    pick = np.concatenate([pick, pick], 0)
    wide = np.arange(TILES * 128)[None, :]
    slot = wide // 128 * 16 + wide % 128 // 8
    spread = [(lane_in == slot) & (wide % 8 == edge) for edge in (0, 7)]
    spread = np.concatenate(spread, 0).astype(jnp.bfloat16)
    tables = (fwd_a, f_low, bwd_a, b_high, coeffs.astype(np.float32), pick)
    return tuple(jnp.asarray(table) for table in tables), jnp.asarray(spread)


def split(value):
    high = value.astype(jnp.bfloat16)
    return high, (value - high.astype(jnp.float32)).astype(jnp.bfloat16)


def dot(a, b):
    return jnp.dot(a, b, preferred_element_type=jnp.float32)


def mirror(value):
    return pltpu.roll(pltpu.roll(value, 64, 1), 4, 0)


def along_z(low, high, coeffs, base):
    sums = []
    for value in (low + high, low - high):
        turned = pltpu.roll(value, 64, 1)
        variants = [value, turned, pltpu.roll(value, 4, 0), pltpu.roll(turned, 4, 0)]
        terms = [coeffs[base + k] * variants[k] for k in range(4)]
        sums.append((terms[0] + terms[1]) + (terms[2] + terms[3]))
        base += 4
    return sums[0] + sums[1], sums[1] - sums[0]


def rank_of(slab, cycle):
    if cycle & (cycle - 1) == 0:
        return slab >> (cycle.bit_length() - 1)
    return lax.div(slab, cycle)


def lanes_from(value, index):
    return jnp.take_along_axis(value, index, axis=1, mode="promise_in_bounds")


def flip(value, sub, lane):
    value = lanes_from(value, lane ^ 7)
    odd = jnp.where(sub % 2 == 0, pltpu.roll(value, 7, 0), pltpu.roll(value, 1, 0))
    return jnp.where(sub % 4 < 2, pltpu.roll(odd, 6, 0), pltpu.roll(odd, 2, 0))


def iotas():
    sub = lax.broadcasted_iota(jnp.int32, (8, 128), 0)
    lane = lax.broadcasted_iota(jnp.int32, (8, 128), 1)
    return sub, lane


def turned_flag(map_ref, row):
    return jnp.broadcast_to(map_ref[pl.ds(row, 1), 0:1], (8, 128)) != 0


def apply_kernel(
    cycle, ids_ref, dev_ref,
    u_ref, m_ref, map_ref, fa_ref, fl_ref, ba_ref, bh_ref, co_ref, pick_ref,
    out_ref, left_ref, right_ref, zed_ref, el_ref, er_ref,
    g_ref, fh_ref, fl2_ref, lz_ref, l_ref, face_ref, pl_ref, pr_ref,
):
    step = pl.program_id(0)
    sub, lane = iotas()
    rows = u_ref.shape[0]
    slabs = rows // 64
    u = u_ref[...].reshape(slabs * EZ, 2, 8, 128)
    v = (u * co_ref[16:18][None]).reshape(rows, 128)
    high, low = split(v)
    uk = jnp.concatenate([high, low], 1)
    g_ref[...] = dot(uk, fa_ref[...]) + dot(high, fl_ref[...])

    for e in range(slabs * EZ):
        base = e * 16
        mbase = e * 48
        low, high = along_z(
            u_ref[base : base + 8, :], mirror(u_ref[base + 8 : base + 16, :]), co_ref, 0
        )
        low = low * m_ref[mbase + 32 : mbase + 40, :]
        high = high * mirror(m_ref[mbase + 40 : mbase + 48, :])
        low, high = along_z(low, high, co_ref, 8)
        lz_ref[base : base + 8, :] = low
        lz_ref[base + 8 : base + 16, :] = mirror(high)
        fx = m_ref[mbase : mbase + 16, :] * g_ref[base : base + 16, :128]
        fy = m_ref[mbase + 16 : mbase + 32, :] * g_ref[base : base + 16, 128:]
        xh, xl = split(fx)
        yh, yl = split(fy)
        fh_ref[base : base + 16, :128] = xh
        fh_ref[base : base + 16, 128:] = yh
        fl2_ref[base : base + 16, :128] = xl
        fl2_ref[base : base + 16, 128:] = yl
    both = dot(fh_ref[...], ba_ref[...])
    l_ref[...] = both[:, :128] + both[:, 128:] + dot(fl2_ref[...], bh_ref[...]) + lz_ref[...]

    b = lane // 8 % 8
    ey = sub % 4
    after_mask = (b == 7) & (ey < 3)
    before_mask = (b == 0) & (ey > 0)
    high_c = (sub >= 4) & (lane >= 64)
    low_c = (sub < 4) & (lane < 64)
    slot = lane // 16
    slot8 = lane // 8
    for s in range(slabs):
        tiles = []
        for k in range(TILES):
            row = s * 64 + k * 8
            t = l_ref[row : row + 8, :]
            after = pltpu.roll(pltpu.roll(t, 56, 1), 7, 0)
            before = pltpu.roll(pltpu.roll(t, 72, 1), 1, 0)
            tiles.append(
                t + jnp.where(after_mask, after, 0.0) + jnp.where(before_mask, before, 0.0)
            )
        for e in range(EZ - 1):
            top = tiles[2 * e + 1]
            bottom = tiles[2 * e + 2]
            tiles[2 * e + 1] = top + jnp.where(
                high_c, pltpu.roll(pltpu.roll(bottom, 64, 1), 4, 0), 0.0
            )
            tiles[2 * e + 2] = bottom + jnp.where(
                low_c, pltpu.roll(pltpu.roll(top, 64, 1), 4, 0), 0.0
            )
        for k in range(TILES):
            row = s * 64 + k * 8
            out_ref[row : row + 8, :] = tiles[k]
        zed = jnp.where(sub < 4, tiles[0], tiles[TILES - 1])
        if s % 2 == 0:
            even = zed
        else:
            odd = pltpu.roll(zed, 64, 1)
            zed_ref[s // 2 * 8 : s // 2 * 8 + 8, :] = jnp.where(
                (sub < 4) == (lane < 64), even, odd
            )
    high, low = split(out_ref[...])
    face_ref[...] = dot(jnp.concatenate([high, low], 1), pick_ref[...])
    for s in range(slabs):
        row = s * 64
        left = face_ref[row : row + 8, :128]
        right = face_ref[row : row + 8, 128:]
        for k in range(1, TILES):
            row = s * 64 + k * 8
            left = jnp.where(slot == k, face_ref[row : row + 8, :128], left)
            right = jnp.where(slot == k, face_ref[row : row + 8, 128:], right)
        position = step * slabs + s
        flag = turned_flag(map_ref, position)
        right = jnp.where(flag, flip(right, sub, lane), right)
        rank = rank_of(ids_ref[dev_ref[0] + position], cycle)
        where = pl.ds(pl.multiple_of(rank * 8, 8), 8)
        left_ref[where, :] = left
        right_ref[where, :] = right
        place = rank & 15
        mask = ((slot8 == place) & (sub < 4)) | ((slot8 == ((place + 15) & 15)) & (sub >= 4))
        pl_ref[where, :] = jnp.where(mask, pltpu.roll(left, place * 8, 1), 0.0)
        pr_ref[where, :] = jnp.where(mask, pltpu.roll(right, place * 8, 1), 0.0)

    @pl.when(step == pl.num_programs(0) - 1)
    def _():
        for from_ref, to_ref in ((pl_ref, el_ref), (pr_ref, er_ref)):
            parts = from_ref[...].reshape(-1, 16, 8, 128)
            to_ref[...] = jnp.sum(parts, axis=1).reshape(to_ref.shape)


def fix_kernel(
    cycle, total, ids_ref, dev_ref,
    in_ref, map_ref, fprev_ref, fnext_ref, zed_ref, eprev_ref, enext_ref, spread_ref,
    out_ref, x_ref, y_ref,
):
    step = pl.program_id(0)
    sub, lane = iotas()
    slabs = in_ref.shape[0] // 64
    low_c = (sub < 4) & (lane < 64)
    high_c = (sub >= 4) & (lane >= 64)
    low_edge = (sub < 4) & (lane < 8)
    high_edge = (sub >= 4) & (lane >= 120)

    def incoming(face_ref, edge_ref, j):
        face = face_ref[pl.ds(pl.multiple_of(j * 8, 8), 8), :]
        edge = edge_ref[pl.ds(pl.multiple_of((j >> 4) * 8, 8), 8), :]
        shift = ((16 - (j & 15)) & 15) * 8
        edge = pltpu.roll(pltpu.roll(edge, shift, 1), 4, 0)
        edge = jnp.where(
            low_edge,
            pltpu.roll(edge, 8, 1),
            jnp.where(high_edge, pltpu.roll(edge, 120, 1), 0.0),
        )
        return face + edge

    half = slabs * 8
    for s in range(slabs):
        p = step * slabs + s
        own = ids_ref[dev_ref[0] + p]
        before = jnp.where(own == 0, total - 1, own - 1)
        after = jnp.where(own == total - 1, 0, own + 1)
        left = incoming(fprev_ref, eprev_ref, rank_of(before, cycle))
        right = incoming(fnext_ref, enext_ref, rank_of(after, cycle))
        right = jnp.where(turned_flag(map_ref, p), flip(right, sub, lane), right)
        x_ref[s * 8 : s * 8 + 8, :128] = left
        x_ref[s * 8 : s * 8 + 8, 128:] = right
    high, low = split(x_ref[...])
    both = dot(jnp.concatenate([high, low], 0), spread_ref[...])
    y_ref[...] = both[:half] + both[half:]
    for s in range(slabs):
        zed = pltpu.roll(zed_ref[s // 2 * 8 : s // 2 * 8 + 8, :], 4, 0)
        if s % 2 == 0:
            zed = pltpu.roll(zed, 64, 1)
        for k in range(TILES):
            row = s * 64 + k * 8
            t = in_ref[row : row + 8, :] + y_ref[s * 8 : s * 8 + 8, k * 128 : k * 128 + 128]
            if k == 0:
                t = t + jnp.where(low_c, zed, 0.0)
            if k == TILES - 1:
                t = t + jnp.where(high_c, zed, 0.0)
            out_ref[row : row + 8, :] = t


def whole_of(array):
    return pl.BlockSpec(array.shape, lambda i, *_: (0,) * array.ndim)


def apply_local(ids, dev, u, m, face_map, tables, cycle):
    slab_count = face_map.shape[0]
    steps = slab_count // BLOCK
    rows = BLOCK * 64
    f32 = jnp.float32
    shapes = [
        (slab_count * 64, 128),
        (slab_count * 8, 128),
        (slab_count * 8, 128),
        (slab_count * 4, 128),
        (slab_count // 2, 128),
        (slab_count // 2, 128),
    ]
    row_block = lambda n: pl.BlockSpec((n, 128), lambda i, *_: (i, 0))
    whole = lambda shape: pl.BlockSpec(shape, lambda i, *_: (0, 0))
    return pl.pallas_call(
        functools.partial(apply_kernel, cycle),
        grid_spec=pltpu.PrefetchScalarGridSpec(
            num_scalar_prefetch=2,
            grid=(steps,),
            in_specs=[row_block(rows), row_block(rows * 3), whole((slab_count, 128))]
            + [whole_of(t) for t in tables],
            out_specs=[
                row_block(rows),
                whole(shapes[1]),
                whole(shapes[2]),
                row_block(BLOCK * 4),
                whole(shapes[4]),
                whole(shapes[5]),
            ],
            scratch_shapes=[
                pltpu.VMEM((rows, 256), f32),
                pltpu.VMEM((rows, 256), jnp.bfloat16),
                pltpu.VMEM((rows, 256), jnp.bfloat16),
                pltpu.VMEM((rows, 128), f32),
                pltpu.VMEM((rows, 128), f32),
                pltpu.VMEM((rows, 256), f32),
                pltpu.VMEM(shapes[1], f32),
                pltpu.VMEM(shapes[1], f32),
            ],
        ),
        out_shape=[jax.ShapeDtypeStruct(s, f32) for s in shapes],
        name="apply_local",
    )(ids, dev, u, m, face_map, *tables)


def fix_faces(ids, dev, local, face_map, fprev, fnext, zed, eprev, enext, spread, cycle):
    slab_count = face_map.shape[0]
    steps = slab_count // FIX_BLOCK
    rows = FIX_BLOCK * 64
    return pl.pallas_call(
        functools.partial(fix_kernel, cycle, slab_count * cycle),
        grid_spec=pltpu.PrefetchScalarGridSpec(
            num_scalar_prefetch=2,
            grid=(steps,),
            in_specs=[
                pl.BlockSpec((rows, 128), lambda i, *_: (i, 0)),
                pl.BlockSpec((slab_count, 128), lambda i, *_: (0, 0)),
                whole_of(fprev),
                whole_of(fnext),
                pl.BlockSpec((FIX_BLOCK * 4, 128), lambda i, *_: (i, 0)),
                whole_of(eprev),
                whole_of(enext),
                whole_of(spread),
            ],
            out_specs=pl.BlockSpec((rows, 128), lambda i, *_: (i, 0)),
            scratch_shapes=[
                pltpu.VMEM((FIX_BLOCK * 8, 256), jnp.float32),
                pltpu.VMEM((FIX_BLOCK * 8, TILES * 128), jnp.float32),
            ],
        ),
        out_shape=jax.ShapeDtypeStruct(local.shape, jnp.float32),
        name="fix_faces",
    )(ids, dev, local, face_map, fprev, fnext, zed, eprev, enext, spread)


def send(value, by, across):
    slabs = lax.axis_size("slab")
    layers = lax.axis_size("layer")
    pairs = [
        (s * layers + l, (s + by) % slabs * layers + (l + across) % layers)
        for s in range(slabs)
        for l in range(layers)
    ]
    return lax.ppermute(value, ("slab", "layer"), pairs)


def body(nodal_field, metric, slab_ids, face_map):
    slab_count = nodal_field.shape[1]
    cycle_size = lax.axis_size("slab")
    first = lax.axis_index("slab").reshape(1) * slab_count
    tables, spread = kernel_tables()
    u = nodal_field.reshape(slab_count, EZ, EY, 4, 128).transpose(0, 1, 3, 2, 4)
    u = u.reshape(slab_count * 64, 128)
    m = metric.reshape(slab_count, EZ, EY, 3, 4, 128).transpose(0, 1, 3, 4, 2, 5)
    m = m.reshape(slab_count * 192, 128)
    local, left, right, zed, edge_left, edge_right = apply_local(
        slab_ids, first, u, m, face_map, tables, cycle_size
    )
    zed = send(zed, 0, 1)
    fprev = send(right, 1, 0)
    fnext = send(left, -1, 0)
    eprev = send(edge_right, 1, 1)
    enext = send(edge_left, -1, 1)

    out = fix_faces(
        slab_ids, first, local, face_map, fprev, fnext, zed, eprev, enext, spread, cycle_size
    )
    out = out.reshape(slab_count, EZ, 4, EY, 128).transpose(0, 1, 3, 2, 4)
    return out.reshape(1, slab_count, EZ, EY, PTS)


def solution(mesh):
    return jax.shard_map(
        body,
        mesh=mesh,
        in_specs=(
            P("layer", "slab", None, None, None),
            P("layer", "slab", None, None, None, None),
            P(),
            P("slab", None),
        ),
        out_specs=P("layer", "slab", None, None, None),
        check_vma=False,
    )
```

time: 43.1 us -> 34.4 us (0.80)
  Pallas kernels: 25.8 us -> 18.6 us
  other arithmetic: 1.63 us -> 0 us
    pallas_call x2, Pallas kernels: 25.8 us -> 18.6 us  [the longest x1 12.6 us: apply_local(): pl.pallas_call(functools.partial(apply_kernel, cycle), grid_spec=pltpu.Pr...]
    select_n x1 -> x0, other arithmetic: 0.88 us -> none  [body(): next_index = index_of(ids_of(device + 1), (own_ids + 1) % total_slabs)]
    reduce_sum x1 -> x0, other arithmetic: 0.75 us -> none  [index_of(): return jnp.sum(jnp.where(hit, position, 0), axis=1)]
  transfers between devices with their start and end apart: 5 -> 5, of which waited for: 1 -> 1; matrix products, arithmetic and copies ran while one was open for 4% -> 0% of each run, Pallas kernels for 0% -> 0%
where the time goes in v2:
time: 34.4 us; the launch traced here: 33.9 us
  Pallas kernels  18.6 us (54%)
  starting transfers between devices  12.8 us (37%)
  waiting for transfers between devices  1.66 us (5%)
  local copies, waits for them, and re-layouts  0.83 us (2%)
    ppermute x5, starting transfers between devices, send(): return lax.ppermute(value, ('slab', 'layer'), pairs)  12.8 us
    pallas_call x1, Pallas kernels, apply_local(): pl.pallas_call(functools.partial(apply_kernel, cycle), grid_spec=pltpu.Pr...  12.6 us
    pallas_call x1, Pallas kernels, fix_faces(): pl.pallas_call(functools.partial(fix_kernel, cycle, slab_count * cycle),...  5.9 us
    ppermute x5, waiting for transfers between devices, send(): return lax.ppermute(value, ('slab', 'layer'), pairs)  1.66 us
    unnamed x10, local copies, waits for them, and re-layouts  0.83 us
  transfers between devices with their start and end apart: 5, of which 1 were waited for; matrix products, arithmetic and copies ran while one was open for 0% of the time, Pallas kernels for 0%

profile of v2, /device:TPU:0, one launch (start us, length us, event | category | flops | bytes accessed | tf_op | source)
XLA Modules:
  0.0 33.9 jit_solution(609960849055337083)
XLA Ops:
  0.0 12.6 %apply_local.1 = (f32[4096,128]{1,0:T(8,128)}, f32[512,128]{1,0:T(8,128)}, f32[512,128]{1,0:T(8,128)}, f32[256,128]{1,0:T(8,128)}, f32[32,128]{1,0:T(8,128)}, /*index=5*/f32[32,128]{1,0:T(8,128)}) custom-call(s32[1024]{0:T(1024)} %ids_ref.3, s32[1]{0:T(128)} %bitcast.dev_ref, f32[4096,128]{1,0:T(8,128)} %bitcast.17, f32[12288,128]{1,0:T(8,128)} %bitcast.16, ...), custom_call_target="tpu_custom_call" | custom-call | tf_op jit(solution)/shard_map/apply_local/pallas_call | solution.py:324
  12.7 0.5 %collective-permute-start = (f32[512,128]{1,0:T(8,128)}, f32[512,128]{1,0:T(8,128)S(1)}, u32[]{:S(2)}, u32[]{:S(2)}) collective-permute-start(f32[512,128]{1,0:T(8,128)} %get-tuple-element.12), channel_id=1, source_target_pairs={{0,2},{1,3},{2,4},{3,5},{4,6},{5,7},{6,8},{7,9},{8,10},{9,11},{10,... | collective-permute-start | bytes 786440 | tf_op jit(solution)/shard_map/ppermute | solution.py:393
  13.2 5.0 %collective-permute-start.1 = (f32[512,128]{1,0:T(8,128)}, f32[512,128]{1,0:T(8,128)S(1)}, u32[]{:S(2)}, u32[]{:S(2)}) collective-permute-start(f32[512,128]{1,0:T(8,128)} %get-tuple-element.13), channel_id=1, source_target_pairs={{0,30},{1,31},{2,0},{3,1},{4,2},{5,3},{6,4},{7,5},{8,6},{9,7},{10,... | collective-permute-start | bytes 786440 | tf_op jit(solution)/shard_map/ppermute | solution.py:393
  18.2 1.9 %collective-permute-start.2 = (f32[256,128]{1,0:T(8,128)}, f32[256,128]{1,0:T(8,128)S(1)}, u32[]{:S(2)}, u32[]{:S(2)}) collective-permute-start(f32[256,128]{1,0:T(8,128)} %get-tuple-element.14), channel_id=1, source_target_pairs={{0,1},{1,0},{2,3},{3,2},{4,5},{5,4},{6,7},{7,6},{8,9},{9,8},{10,11... | collective-permute-start | bytes 393224 | tf_op jit(solution)/shard_map/ppermute | solution.py:393
  20.1 0.0 collective-permute-start.3
  20.1 5.3 %collective-permute-start.4 = (f32[32,128]{1,0:T(8,128)}, f32[32,128]{1,0:T(8,128)S(1)}, u32[]{:S(2)}, u32[]{:S(2)}) collective-permute-start(f32[32,128]{1,0:T(8,128)} %get-tuple-element.16), channel_id=1, source_target_pairs={{0,31},{1,30},{2,1},{3,0},{4,3},{5,2},{6,5},{7,4},{8,7},{9,6},{10,... | collective-permute-start | bytes 49160 | tf_op jit(solution)/shard_map/ppermute | solution.py:393
  25.5 1.6 %collective-permute-done.3.eprev_ref = f32[32,128]{1,0:T(8,128)S(1)} collective-permute-done((f32[32,128]{1,0:T(8,128)}, f32[32,128]{1,0:T(8,128)S(1)}, u32[]{:S(2)}, u32[]{:S(2)}) %collective-permute-start.3) | collective-permute-done | bytes 16416 | tf_op jit(solution)/shard_map/ppermute | solution.py:393
  27.1 0.0 copy-start.3
  27.1 0.0 collective-permute-done.4.enext_ref
  27.1 0.0 copy-start.4
  27.1 0.0 collective-permute-done.2.zed_ref
  27.1 0.0 copy-start.2
  27.2 0.0 collective-permute-done.fprev_ref
  27.2 0.0 copy-start
  27.2 0.0 collective-permute-done.1.fnext_ref
  27.2 0.0 copy-start.1
  27.2 0.5 %copy-done.3 = f32[32,128]{1,0:T(8,128)} copy-done((f32[32,128]{1,0:T(8,128)}, f32[32,128]{1,0:T(8,128)S(1)}, u32[]{:S(2)}) %copy-start.3) | copy-done | bytes 16408
  27.7 0.0 copy-done.4
  27.7 0.1 copy-done.2
  27.8 0.1 copy-done
  27.9 0.1 copy-done.1
  28.0 5.9 %fix_faces.1 = f32[4096,128]{1,0:T(8,128)} custom-call(s32[1024]{0:T(1024)} %ids_ref.3, s32[1]{0:T(128)} %bitcast.dev_ref, f32[4096,128]{1,0:T(8,128)} %get-tuple-element.11.in_ref, s32[64,1024]{1,0:T(8,128)} %map_ref.3, f32[512,128]{1,0:T(8,128)} %copy-done, f32[512,128]{1,0:T(8,128)} %copy-done.1, f32[256,128]{1,0:T(8,128)} %copy-done.2, ...), custom_call_target="tpu_custom_call" | custom-call | tf_op jit(solution)/shard_map/fix_faces/pallas_call | solution.py:359
Async XLA Ops:
  12.7 14.5 %collective-permute-start = (f32[512,128]{1,0:T(8,128)}, f32[512,128]{1,0:T(8,128)S(1)}, u32[]{:S(2)}, u32[]{:S(2)}) collective-permute-start(f32[512,128]{1,0:T(8,128)} %get-tuple-element.12), channel_id=1, source_target_pairs={{0,2},{1,3},{2,4},{3,5},{4,6},{5,7},{6,8},{7,9},{8,10},{9,11},{10,... | collective-permute-start | bytes 786440 | tf_op jit(solution)/shard_map/ppermute | solution.py:393
  13.2 14.0 %collective-permute-start.1 = (f32[512,128]{1,0:T(8,128)}, f32[512,128]{1,0:T(8,128)S(1)}, u32[]{:S(2)}, u32[]{:S(2)}) collective-permute-start(f32[512,128]{1,0:T(8,128)} %get-tuple-element.13), channel_id=1, source_target_pairs={{0,30},{1,31},{2,0},{3,1},{4,2},{5,3},{6,4},{7,5},{8,6},{9,7},{10,... | collective-permute-start | bytes 786440 | tf_op jit(solution)/shard_map/ppermute | solution.py:393
  18.2 8.9 %collective-permute-start.2 = (f32[256,128]{1,0:T(8,128)}, f32[256,128]{1,0:T(8,128)S(1)}, u32[]{:S(2)}, u32[]{:S(2)}) collective-permute-start(f32[256,128]{1,0:T(8,128)} %get-tuple-element.14), channel_id=1, source_target_pairs={{0,1},{1,0},{2,3},{3,2},{4,5},{5,4},{6,7},{7,6},{8,9},{9,8},{10,11... | collective-permute-start | bytes 393224 | tf_op jit(solution)/shard_map/ppermute | solution.py:393
  20.1 7.0 %collective-permute-start.3 = (f32[32,128]{1,0:T(8,128)}, f32[32,128]{1,0:T(8,128)S(1)}, u32[]{:S(2)}, u32[]{:S(2)}) collective-permute-start(f32[32,128]{1,0:T(8,128)} %get-tuple-element.15), channel_id=1, source_target_pairs={{0,3},{1,2},{2,5},{3,4},{4,7},{5,6},{6,9},{7,8},{8,11},{9,10},{10,... | collective-permute-start | bytes 49160 | tf_op jit(solution)/shard_map/ppermute | solution.py:393
  20.1 7.0 %collective-permute-start.4 = (f32[32,128]{1,0:T(8,128)}, f32[32,128]{1,0:T(8,128)S(1)}, u32[]{:S(2)}, u32[]{:S(2)}) collective-permute-start(f32[32,128]{1,0:T(8,128)} %get-tuple-element.16), channel_id=1, source_target_pairs={{0,31},{1,30},{2,1},{3,0},{4,3},{5,2},{6,5},{7,4},{8,7},{9,6},{10,... | collective-permute-start | bytes 49160 | tf_op jit(solution)/shard_map/ppermute | solution.py:393
  27.1 0.6 %copy-start.3 = (f32[32,128]{1,0:T(8,128)}, f32[32,128]{1,0:T(8,128)S(1)}, u32[]{:S(2)}) copy-start(f32[32,128]{1,0:T(8,128)S(1)} %collective-permute-done.3.eprev_ref) | copy-start | bytes 49156
  27.1 0.6 %copy-start.4 = (f32[32,128]{1,0:T(8,128)}, f32[32,128]{1,0:T(8,128)S(1)}, u32[]{:S(2)}) copy-start(f32[32,128]{1,0:T(8,128)S(1)} %collective-permute-done.4.enext_ref) | copy-start | bytes 49156
  27.1 0.7 %copy-start.2 = (f32[256,128]{1,0:T(8,128)}, f32[256,128]{1,0:T(8,128)S(1)}, u32[]{:S(2)}) copy-start(f32[256,128]{1,0:T(8,128)S(1)} %collective-permute-done.2.zed_ref) | copy-start | bytes 393220
  27.2 0.8 %copy-start = (f32[512,128]{1,0:T(8,128)}, f32[512,128]{1,0:T(8,128)S(1)}, u32[]{:S(2)}) copy-start(f32[512,128]{1,0:T(8,128)S(1)} %collective-permute-done.fprev_ref) | copy-start | bytes 786436
  27.2 0.8 %copy-start.1 = (f32[512,128]{1,0:T(8,128)}, f32[512,128]{1,0:T(8,128)S(1)}, u32[]{:S(2)}) copy-start(f32[512,128]{1,0:T(8,128)S(1)} %collective-permute-done.1.fnext_ref) | copy-start | bytes 786436

commit v3 on v2

--- a/solution.py
+++ b/solution.py
@@ -147,7 +147,7 @@
 def apply_kernel(
     cycle, ids_ref, dev_ref,
     u_ref, m_ref, map_ref, fa_ref, fl_ref, ba_ref, bh_ref, co_ref, pick_ref,
-    out_ref, left_ref, right_ref, zed_ref, el_ref, er_ref,
+    out_ref, left_ref, right_ref, swap_ref,
     g_ref, fh_ref, fl2_ref, lz_ref, l_ref, face_ref, pl_ref, pr_ref,
 ):
     step = pl.program_id(0)
@@ -217,9 +217,8 @@
             even = zed
         else:
             odd = pltpu.roll(zed, 64, 1)
-            zed_ref[s // 2 * 8 : s // 2 * 8 + 8, :] = jnp.where(
-                (sub < 4) == (lane < 64), even, odd
-            )
+            where = pl.ds(pl.multiple_of((step * slabs + s - 1) * 4, 8), 8)
+            swap_ref[where, :] = jnp.where((sub < 4) == (lane < 64), even, odd)
     high, low = split(out_ref[...])
     face_ref[...] = dot(jnp.concatenate([high, low], 1), pick_ref[...])
     for s in range(slabs):
@@ -244,14 +243,35 @@
 
     @pl.when(step == pl.num_programs(0) - 1)
     def _():
-        for from_ref, to_ref in ((pl_ref, el_ref), (pr_ref, er_ref)):
+        count = pl_ref.shape[0] // 16
+        base = pl_ref.shape[0] // 2
+        for from_ref in (pl_ref, pr_ref):
             parts = from_ref[...].reshape(-1, 16, 8, 128)
-            to_ref[...] = jnp.sum(parts, axis=1).reshape(to_ref.shape)
+            swap_ref[base : base + count, :] = jnp.sum(parts, axis=1).reshape(count, 128)
+            base += count
+
+
+def edge_kernel(left_ref, right_ref, swap_ref, left_out, right_out):
+    sub, lane = iotas()
+    low_edge = (sub < 4) & (lane < 8)
+    high_edge = (sub >= 4) & (lane >= 120)
+    slabs = left_ref.shape[0] // 8
+    base = slabs * 4
+    for face_ref, to_ref in ((left_ref, left_out), (right_ref, right_out)):
+        for s in range(slabs):
+            place = s % 16
+            if place == 0:
+                edge = pltpu.roll(swap_ref[base + s // 2 : base + s // 2 + 8, :], 4, 0)
+            low = pltpu.roll(edge, (136 - 8 * place) % 128, 1)
+            high = pltpu.roll(edge, 120 - 8 * place, 1)
+            other = jnp.where(low_edge, low, jnp.where(high_edge, high, 0.0))
+            to_ref[s * 8 : s * 8 + 8, :] = face_ref[s * 8 : s * 8 + 8, :] + other
+        base += slabs // 2
 
 
 def fix_kernel(
     cycle, total, ids_ref, dev_ref,
-    in_ref, map_ref, fprev_ref, fnext_ref, zed_ref, eprev_ref, enext_ref, spread_ref,
+    in_ref, map_ref, fprev_ref, fnext_ref, zed_ref, spread_ref,
     out_ref, x_ref, y_ref,
 ):
     step = pl.program_id(0)
@@ -259,20 +279,9 @@
     slabs = in_ref.shape[0] // 64
     low_c = (sub < 4) & (lane < 64)
     high_c = (sub >= 4) & (lane >= 64)
-    low_edge = (sub < 4) & (lane < 8)
-    high_edge = (sub >= 4) & (lane >= 120)
-
-    def incoming(face_ref, edge_ref, j):
-        face = face_ref[pl.ds(pl.multiple_of(j * 8, 8), 8), :]
-        edge = edge_ref[pl.ds(pl.multiple_of((j >> 4) * 8, 8), 8), :]
-        shift = ((16 - (j & 15)) & 15) * 8
-        edge = pltpu.roll(pltpu.roll(edge, shift, 1), 4, 0)
-        edge = jnp.where(
-            low_edge,
-            pltpu.roll(edge, 8, 1),
-            jnp.where(high_edge, pltpu.roll(edge, 120, 1), 0.0),
-        )
-        return face + edge
+
+    def incoming(face_ref, rank):
+        return face_ref[pl.ds(pl.multiple_of(rank * 8, 8), 8), :]
 
     half = slabs * 8
     for s in range(slabs):
@@ -280,8 +289,8 @@
         own = ids_ref[dev_ref[0] + p]
         before = jnp.where(own == 0, total - 1, own - 1)
         after = jnp.where(own == total - 1, 0, own + 1)
-        left = incoming(fprev_ref, eprev_ref, rank_of(before, cycle))
-        right = incoming(fnext_ref, enext_ref, rank_of(after, cycle))
+        left = incoming(fprev_ref, rank_of(before, cycle))
+        right = incoming(fnext_ref, rank_of(after, cycle))
         right = jnp.where(turned_flag(map_ref, p), flip(right, sub, lane), right)
         x_ref[s * 8 : s * 8 + 8, :128] = left
         x_ref[s * 8 : s * 8 + 8, 128:] = right
@@ -315,9 +324,7 @@
         (slab_count * 64, 128),
         (slab_count * 8, 128),
         (slab_count * 8, 128),
-        (slab_count * 4, 128),
-        (slab_count // 2, 128),
-        (slab_count // 2, 128),
+        (slab_count * 5, 128),
     ]
     row_block = lambda n: pl.BlockSpec((n, 128), lambda i, *_: (i, 0))
     whole = lambda shape: pl.BlockSpec(shape, lambda i, *_: (0, 0))
@@ -332,9 +339,7 @@
                 row_block(rows),
                 whole(shapes[1]),
                 whole(shapes[2]),
-                row_block(BLOCK * 4),
-                whole(shapes[4]),
-                whole(shapes[5]),
+                whole(shapes[3]),
             ],
             scratch_shapes=[
                 pltpu.VMEM((rows, 256), f32),
@@ -352,7 +357,15 @@
     )(ids, dev, u, m, face_map, *tables)
 
 
-def fix_faces(ids, dev, local, face_map, fprev, fnext, zed, eprev, enext, spread, cycle):
+def add_edges(left, right, swap):
+    return pl.pallas_call(
+        edge_kernel,
+        out_shape=[jax.ShapeDtypeStruct(left.shape, jnp.float32)] * 2,
+        name="add_edges",
+    )(left, right, swap)
+
+
+def fix_faces(ids, dev, local, face_map, fprev, fnext, zed, spread, cycle):
     slab_count = face_map.shape[0]
     steps = slab_count // FIX_BLOCK
     rows = FIX_BLOCK * 64
@@ -367,8 +380,6 @@
                 whole_of(fprev),
                 whole_of(fnext),
                 pl.BlockSpec((FIX_BLOCK * 4, 128), lambda i, *_: (i, 0)),
-                whole_of(eprev),
-                whole_of(enext),
                 whole_of(spread),
             ],
             out_specs=pl.BlockSpec((rows, 128), lambda i, *_: (i, 0)),
@@ -379,7 +390,7 @@
         ),
         out_shape=jax.ShapeDtypeStruct(local.shape, jnp.float32),
         name="fix_faces",
-    )(ids, dev, local, face_map, fprev, fnext, zed, eprev, enext, spread)
+    )(ids, dev, local, face_map, fprev, fnext, zed, spread)
 
 
 def send(value, by, across):
@@ -402,17 +413,15 @@
     u = u.reshape(slab_count * 64, 128)
     m = metric.reshape(slab_count, EZ, EY, 3, 4, 128).transpose(0, 1, 3, 4, 2, 5)
     m = m.reshape(slab_count * 192, 128)
-    local, left, right, zed, edge_left, edge_right = apply_local(
+    local, left, right, swap = apply_local(
         slab_ids, first, u, m, face_map, tables, cycle_size
     )
-    zed = send(zed, 0, 1)
+    swap = send(swap, 0, 1)
+    left, right = add_edges(left, right, swap)
     fprev = send(right, 1, 0)
     fnext = send(left, -1, 0)
-    eprev = send(edge_right, 1, 1)
-    enext = send(edge_left, -1, 1)
-
     out = fix_faces(
-        slab_ids, first, local, face_map, fprev, fnext, zed, eprev, enext, spread, cycle_size
+        slab_ids, first, local, face_map, fprev, fnext, swap, spread, cycle_size
     )
     out = out.reshape(slab_count, EZ, 4, EY, 128).transpose(0, 1, 3, 2, 4)
     return out.reshape(1, slab_count, EZ, EY, PTS)

time: 34.4 us -> 39.7 us (1.15)
  the two profiles are of different devices: /device:TPU:0 before, /device:TPU:1 now
where the time goes in v3:
time: 39.7 us; the launch traced here: 39.2 us
  Pallas kernels  20.2 us (51%)
  waiting for transfers between devices  12.9 us (32%)
  starting transfers between devices  4.69 us (12%)
  local copies, waits for them, and re-layouts  1.38 us (3%)
    ppermute x3, waiting for transfers between devices, send(): return lax.ppermute(value, ('slab', 'layer'), pairs)  12.9 us
    pallas_call x1, Pallas kernels, apply_local(): pl.pallas_call(functools.partial(apply_kernel, cycle), grid_spec=pltpu.Pr...  12.7 us
    pallas_call x1, Pallas kernels, fix_faces(): pl.pallas_call(functools.partial(fix_kernel, cycle, slab_count * cycle),...  5.54 us
    ppermute x3, starting transfers between devices, send(): return lax.ppermute(value, ('slab', 'layer'), pairs)  4.69 us
    pallas_call x1, Pallas kernels, add_edges(): pl.pallas_call(edge_kernel, out_shape=[jax.ShapeDtypeStruct(left.shape, j...  1.99 us
    unnamed x6, local copies, waits for them, and re-layouts  1.38 us
  transfers between devices with their start and end apart: 3, of which 3 were waited for; matrix products, arithmetic and copies ran while one was open for 0% of the time, Pallas kernels for 0%

profile of v3, /device:TPU:1, one launch (start us, length us, event | category | flops | bytes accessed | tf_op | source)
XLA Modules:
  0.0 39.2 jit_solution(16689230405446534458)
XLA Ops:
  0.0 12.7 %apply_local.1 = (f32[4096,128]{1,0:T(8,128)}, f32[512,128]{1,0:T(8,128)}, f32[512,128]{1,0:T(8,128)}, f32[320,128]{1,0:T(8,128)}) custom-call(s32[1024]{0:T(1024)} %ids_ref.3, s32[1]{0:T(128)} %bitcast.dev_ref, f32[4096,128]{1,0:T(8,128)} %bitcast.17, f32[12288,128]{1,0:T(8,128)} %bitcast.16, s32[64,1024]{1,0:T(8,128)} %map_ref.3, ...), custom_call_target="tpu_custom_call" | custom-call | tf_op jit(solution)/shard_map/apply_local/pallas_call | solution.py:331
  12.7 2.1 %collective-permute-start = (f32[320,128]{1,0:T(8,128)}, f32[320,128]{1,0:T(8,128)S(1)}, u32[]{:S(2)}, u32[]{:S(2)}) collective-permute-start(f32[320,128]{1,0:T(8,128)} %get-tuple-element.14), channel_id=1, source_target_pairs={{0,1},{1,0},{2,3},{3,2},{4,5},{5,4},{6,7},{7,6},{8,9},{9,8},{10,11... | collective-permute-start | bytes 491528 | tf_op jit(solution)/shard_map/ppermute | solution.py:404
  14.8 4.1 %collective-permute-done.swap_ref.zed_ref = f32[320,128]{1,0:T(8,128)S(1)} collective-permute-done((f32[320,128]{1,0:T(8,128)}, f32[320,128]{1,0:T(8,128)S(1)}, u32[]{:S(2)}, u32[]{:S(2)}) %collective-permute-start) | collective-permute-done | bytes 163872 | tf_op jit(solution)/shard_map/ppermute | solution.py:404
  18.9 0.0 copy-start
  18.9 0.7 %copy-done = f32[320,128]{1,0:T(8,128)} copy-done((f32[320,128]{1,0:T(8,128)}, f32[320,128]{1,0:T(8,128)S(1)}, u32[]{:S(2)}) %copy-start) | copy-done | bytes 163864
  19.6 2.0 %add_edges.1 = (f32[512,128]{1,0:T(8,128)}, f32[512,128]{1,0:T(8,128)}) custom-call(f32[512,128]{1,0:T(8,128)} %get-tuple-element.12.left_ref, f32[512,128]{1,0:T(8,128)} %get-tuple-element.13.right_ref, f32[320,128]{1,0:T(8,128)} %copy-done), custom_call_target="tpu_custom_call" | custom-call | tf_op jit(solution)/shard_map/add_edges/pallas_call | solution.py:361
  21.6 2.6 %collective-permute-start.1 = (f32[512,128]{1,0:T(8,128)}, f32[512,128]{1,0:T(8,128)S(1)}, u32[]{:S(2)}, u32[]{:S(2)}) collective-permute-start(f32[512,128]{1,0:T(8,128)} %get-tuple-element.15), channel_id=1, source_target_pairs={{0,2},{1,3},{2,4},{3,5},{4,6},{5,7},{6,8},{7,9},{8,10},{9,11},{10,... | collective-permute-start | bytes 786440 | tf_op jit(solution)/shard_map/ppermute | solution.py:404
  24.1 0.0 collective-permute-start.2
  24.1 3.6 %collective-permute-done.1.fprev_ref = f32[512,128]{1,0:T(8,128)S(1)} collective-permute-done((f32[512,128]{1,0:T(8,128)}, f32[512,128]{1,0:T(8,128)S(1)}, u32[]{:S(2)}, u32[]{:S(2)}) %collective-permute-start.1) | collective-permute-done | bytes 262176 | tf_op jit(solution)/shard_map/ppermute | solution.py:404
  27.8 0.0 copy-start.1
  27.8 5.2 %collective-permute-done.2.fnext_ref = f32[512,128]{1,0:T(8,128)S(1)} collective-permute-done((f32[512,128]{1,0:T(8,128)}, f32[512,128]{1,0:T(8,128)S(1)}, u32[]{:S(2)}, u32[]{:S(2)}) %collective-permute-start.2) | collective-permute-done | bytes 262176 | tf_op jit(solution)/shard_map/ppermute | solution.py:404
  32.9 0.0 copy-start.2
  32.9 0.0 copy-done.1
  32.9 0.7 %copy-done.2 = f32[512,128]{1,0:T(8,128)} copy-done((f32[512,128]{1,0:T(8,128)}, f32[512,128]{1,0:T(8,128)S(1)}, u32[]{:S(2)}) %copy-start.2) | copy-done | bytes 262168
  33.6 5.5 %fix_faces.1 = f32[4096,128]{1,0:T(8,128)} custom-call(s32[1024]{0:T(1024)} %ids_ref.3, s32[1]{0:T(128)} %bitcast.dev_ref, f32[4096,128]{1,0:T(8,128)} %get-tuple-element.11.in_ref, s32[64,1024]{1,0:T(8,128)} %map_ref.3, f32[512,128]{1,0:T(8,128)} %copy-done.1, f32[512,128]{1,0:T(8,128)} %copy-done.2, f32[320,128]{1,0:T(8,128)} %copy-done, ...), custom_call_target="tpu_custom_call" | custom-call | tf_op jit(solution)/shard_map/fix_faces/pallas_call | solution.py:372
Async XLA Ops:
  12.7 6.2 %collective-permute-start = (f32[320,128]{1,0:T(8,128)}, f32[320,128]{1,0:T(8,128)S(1)}, u32[]{:S(2)}, u32[]{:S(2)}) collective-permute-start(f32[320,128]{1,0:T(8,128)} %get-tuple-element.14), channel_id=1, source_target_pairs={{0,1},{1,0},{2,3},{3,2},{4,5},{5,4},{6,7},{7,6},{8,9},{9,8},{10,11... | collective-permute-start | bytes 491528 | tf_op jit(solution)/shard_map/ppermute | solution.py:404
  18.9 0.7 %copy-start = (f32[320,128]{1,0:T(8,128)}, f32[320,128]{1,0:T(8,128)S(1)}, u32[]{:S(2)}) copy-start(f32[320,128]{1,0:T(8,128)S(1)} %collective-permute-done.swap_ref.zed_ref) | copy-start | bytes 491524
  21.6 6.2 %collective-permute-start.1 = (f32[512,128]{1,0:T(8,128)}, f32[512,128]{1,0:T(8,128)S(1)}, u32[]{:S(2)}, u32[]{:S(2)}) collective-permute-start(f32[512,128]{1,0:T(8,128)} %get-tuple-element.15), channel_id=1, source_target_pairs={{0,2},{1,3},{2,4},{3,5},{4,6},{5,7},{6,8},{7,9},{8,10},{9,11},{10,... | collective-permute-start | bytes 786440 | tf_op jit(solution)/shard_map/ppermute | solution.py:404
  24.1 8.8 %collective-permute-start.2 = (f32[512,128]{1,0:T(8,128)}, f32[512,128]{1,0:T(8,128)S(1)}, u32[]{:S(2)}, u32[]{:S(2)}) collective-permute-start(f32[512,128]{1,0:T(8,128)} %get-tuple-element.16), channel_id=1, source_target_pairs={{0,30},{1,31},{2,0},{3,1},{4,2},{5,3},{6,4},{7,5},{8,6},{9,7},{10,... | collective-permute-start | bytes 786440 | tf_op jit(solution)/shard_map/ppermute | solution.py:404
  27.8 5.2 %copy-start.1 = (f32[512,128]{1,0:T(8,128)}, f32[512,128]{1,0:T(8,128)S(1)}, u32[]{:S(2)}) copy-start(f32[512,128]{1,0:T(8,128)S(1)} %collective-permute-done.1.fprev_ref) | copy-start | bytes 786436
  32.9 0.7 %copy-start.2 = (f32[512,128]{1,0:T(8,128)}, f32[512,128]{1,0:T(8,128)S(1)}, u32[]{:S(2)}) copy-start(f32[512,128]{1,0:T(8,128)S(1)} %collective-permute-done.2.fnext_ref) | copy-start | bytes 786436

commit v4 on v2

--- a/solution.py
+++ b/solution.py
@@ -14,7 +14,7 @@
 EZ = 4
 TILES = EZ * 2
 BLOCK = 8
-FIX_BLOCK = 16
+FIX_BLOCK = 8
 
 
 def legendre_pair(gll_nodes, degree):

time: 34.4 us -> 36.9 us (1.073)
  Pallas kernels: 18.6 us -> 21 us
    pallas_call x1, Pallas kernels: 5.9 us -> 8.37 us  [fix_faces(): pl.pallas_call(functools.partial(fix_kernel, cycle, slab_count * cycle),...]
where the time goes in v4:
time: 36.9 us; the launch traced here: 36.4 us
  Pallas kernels  21 us (57%)
  starting transfers between devices  12.8 us (35%)
  waiting for transfers between devices  1.66 us (4%)
  local copies, waits for them, and re-layouts  0.83 us (2%)
    ppermute x5, starting transfers between devices, send(): return lax.ppermute(value, ('slab', 'layer'), pairs)  12.8 us
    pallas_call x1, Pallas kernels, apply_local(): pl.pallas_call(functools.partial(apply_kernel, cycle), grid_spec=pltpu.Pr...  12.6 us
    pallas_call x1, Pallas kernels, fix_faces(): pl.pallas_call(functools.partial(fix_kernel, cycle, slab_count * cycle),...  8.37 us
    ppermute x5, waiting for transfers between devices, send(): return lax.ppermute(value, ('slab', 'layer'), pairs)  1.66 us
    unnamed x10, local copies, waits for them, and re-layouts  0.83 us
  transfers between devices with their start and end apart: 5, of which 1 were waited for; matrix products, arithmetic and copies ran while one was open for 0% of the time, Pallas kernels for 0%

profile of v4, /device:TPU:0, one launch (start us, length us, event | category | flops | bytes accessed | tf_op | source)
XLA Modules:
  0.0 36.4 jit_solution(1686634192098075337)
XLA Ops:
  0.0 12.6 %apply_local.1 = (f32[4096,128]{1,0:T(8,128)}, f32[512,128]{1,0:T(8,128)}, f32[512,128]{1,0:T(8,128)}, f32[256,128]{1,0:T(8,128)}, f32[32,128]{1,0:T(8,128)}, /*index=5*/f32[32,128]{1,0:T(8,128)}) custom-call(s32[1024]{0:T(1024)} %ids_ref.3, s32[1]{0:T(128)} %bitcast.dev_ref, f32[4096,128]{1,0:T(8,128)} %bitcast.17, f32[12288,128]{1,0:T(8,128)} %bitcast.16, ...), custom_call_target="tpu_custom_call" | custom-call | tf_op jit(solution)/shard_map/apply_local/pallas_call | solution.py:324
  12.7 0.5 %collective-permute-start = (f32[512,128]{1,0:T(8,128)}, f32[512,128]{1,0:T(8,128)S(1)}, u32[]{:S(2)}, u32[]{:S(2)}) collective-permute-start(f32[512,128]{1,0:T(8,128)} %get-tuple-element.12), channel_id=1, source_target_pairs={{0,2},{1,3},{2,4},{3,5},{4,6},{5,7},{6,8},{7,9},{8,10},{9,11},{10,... | collective-permute-start | bytes 786440 | tf_op jit(solution)/shard_map/ppermute | solution.py:393
  13.2 5.0 %collective-permute-start.1 = (f32[512,128]{1,0:T(8,128)}, f32[512,128]{1,0:T(8,128)S(1)}, u32[]{:S(2)}, u32[]{:S(2)}) collective-permute-start(f32[512,128]{1,0:T(8,128)} %get-tuple-element.13), channel_id=1, source_target_pairs={{0,30},{1,31},{2,0},{3,1},{4,2},{5,3},{6,4},{7,5},{8,6},{9,7},{10,... | collective-permute-start | bytes 786440 | tf_op jit(solution)/shard_map/ppermute | solution.py:393
  18.2 1.9 %collective-permute-start.2 = (f32[256,128]{1,0:T(8,128)}, f32[256,128]{1,0:T(8,128)S(1)}, u32[]{:S(2)}, u32[]{:S(2)}) collective-permute-start(f32[256,128]{1,0:T(8,128)} %get-tuple-element.14), channel_id=1, source_target_pairs={{0,1},{1,0},{2,3},{3,2},{4,5},{5,4},{6,7},{7,6},{8,9},{9,8},{10,11... | collective-permute-start | bytes 393224 | tf_op jit(solution)/shard_map/ppermute | solution.py:393
  20.1 0.0 collective-permute-start.3
  20.1 5.3 %collective-permute-start.4 = (f32[32,128]{1,0:T(8,128)}, f32[32,128]{1,0:T(8,128)S(1)}, u32[]{:S(2)}, u32[]{:S(2)}) collective-permute-start(f32[32,128]{1,0:T(8,128)} %get-tuple-element.16), channel_id=1, source_target_pairs={{0,31},{1,30},{2,1},{3,0},{4,3},{5,2},{6,5},{7,4},{8,7},{9,6},{10,... | collective-permute-start | bytes 49160 | tf_op jit(solution)/shard_map/ppermute | solution.py:393
  25.5 1.6 %collective-permute-done.3.eprev_ref = f32[32,128]{1,0:T(8,128)S(1)} collective-permute-done((f32[32,128]{1,0:T(8,128)}, f32[32,128]{1,0:T(8,128)S(1)}, u32[]{:S(2)}, u32[]{:S(2)}) %collective-permute-start.3) | collective-permute-done | bytes 16416 | tf_op jit(solution)/shard_map/ppermute | solution.py:393
  27.1 0.0 copy-start.3
  27.1 0.0 collective-permute-done.4.enext_ref
  27.1 0.0 copy-start.4
  27.1 0.0 collective-permute-done.2.zed_ref
  27.1 0.0 copy-start.2
  27.2 0.0 collective-permute-done.fprev_ref
  27.2 0.0 copy-start
  27.2 0.0 collective-permute-done.1.fnext_ref
  27.2 0.0 copy-start.1
  27.2 0.5 %copy-done.3 = f32[32,128]{1,0:T(8,128)} copy-done((f32[32,128]{1,0:T(8,128)}, f32[32,128]{1,0:T(8,128)S(1)}, u32[]{:S(2)}) %copy-start.3) | copy-done | bytes 16408
  27.7 0.0 copy-done.4
  27.7 0.1 copy-done.2
  27.8 0.1 copy-done
  27.9 0.1 copy-done.1
  28.0 8.4 %fix_faces.1 = f32[4096,128]{1,0:T(8,128)} custom-call(s32[1024]{0:T(1024)} %ids_ref.3, s32[1]{0:T(128)} %bitcast.dev_ref, f32[4096,128]{1,0:T(8,128)} %get-tuple-element.11.in_ref, s32[64,1024]{1,0:T(8,128)} %map_ref.3, f32[512,128]{1,0:T(8,128)} %copy-done, f32[512,128]{1,0:T(8,128)} %copy-done.1, f32[256,128]{1,0:T(8,128)} %copy-done.2, ...), custom_call_target="tpu_custom_call" | custom-call | tf_op jit(solution)/shard_map/fix_faces/pallas_call | solution.py:359
Async XLA Ops:
  12.7 14.5 %collective-permute-start = (f32[512,128]{1,0:T(8,128)}, f32[512,128]{1,0:T(8,128)S(1)}, u32[]{:S(2)}, u32[]{:S(2)}) collective-permute-start(f32[512,128]{1,0:T(8,128)} %get-tuple-element.12), channel_id=1, source_target_pairs={{0,2},{1,3},{2,4},{3,5},{4,6},{5,7},{6,8},{7,9},{8,10},{9,11},{10,... | collective-permute-start | bytes 786440 | tf_op jit(solution)/shard_map/ppermute | solution.py:393
  13.2 14.0 %collective-permute-start.1 = (f32[512,128]{1,0:T(8,128)}, f32[512,128]{1,0:T(8,128)S(1)}, u32[]{:S(2)}, u32[]{:S(2)}) collective-permute-start(f32[512,128]{1,0:T(8,128)} %get-tuple-element.13), channel_id=1, source_target_pairs={{0,30},{1,31},{2,0},{3,1},{4,2},{5,3},{6,4},{7,5},{8,6},{9,7},{10,... | collective-permute-start | bytes 786440 | tf_op jit(solution)/shard_map/ppermute | solution.py:393
  18.2 8.9 %collective-permute-start.2 = (f32[256,128]{1,0:T(8,128)}, f32[256,128]{1,0:T(8,128)S(1)}, u32[]{:S(2)}, u32[]{:S(2)}) collective-permute-start(f32[256,128]{1,0:T(8,128)} %get-tuple-element.14), channel_id=1, source_target_pairs={{0,1},{1,0},{2,3},{3,2},{4,5},{5,4},{6,7},{7,6},{8,9},{9,8},{10,11... | collective-permute-start | bytes 393224 | tf_op jit(solution)/shard_map/ppermute | solution.py:393
  20.1 7.0 %collective-permute-start.3 = (f32[32,128]{1,0:T(8,128)}, f32[32,128]{1,0:T(8,128)S(1)}, u32[]{:S(2)}, u32[]{:S(2)}) collective-permute-start(f32[32,128]{1,0:T(8,128)} %get-tuple-element.15), channel_id=1, source_target_pairs={{0,3},{1,2},{2,5},{3,4},{4,7},{5,6},{6,9},{7,8},{8,11},{9,10},{10,... | collective-permute-start | bytes 49160 | tf_op jit(solution)/shard_map/ppermute | solution.py:393
  20.1 7.0 %collective-permute-start.4 = (f32[32,128]{1,0:T(8,128)}, f32[32,128]{1,0:T(8,128)S(1)}, u32[]{:S(2)}, u32[]{:S(2)}) collective-permute-start(f32[32,128]{1,0:T(8,128)} %get-tuple-element.16), channel_id=1, source_target_pairs={{0,31},{1,30},{2,1},{3,0},{4,3},{5,2},{6,5},{7,4},{8,7},{9,6},{10,... | collective-permute-start | bytes 49160 | tf_op jit(solution)/shard_map/ppermute | solution.py:393
  27.1 0.6 %copy-start.3 = (f32[32,128]{1,0:T(8,128)}, f32[32,128]{1,0:T(8,128)S(1)}, u32[]{:S(2)}) copy-start(f32[32,128]{1,0:T(8,128)S(1)} %collective-permute-done.3.eprev_ref) | copy-start | bytes 49156
  27.1 0.6 %copy-start.4 = (f32[32,128]{1,0:T(8,128)}, f32[32,128]{1,0:T(8,128)S(1)}, u32[]{:S(2)}) copy-start(f32[32,128]{1,0:T(8,128)S(1)} %collective-permute-done.4.enext_ref) | copy-start | bytes 49156
  27.1 0.7 %copy-start.2 = (f32[256,128]{1,0:T(8,128)}, f32[256,128]{1,0:T(8,128)S(1)}, u32[]{:S(2)}) copy-start(f32[256,128]{1,0:T(8,128)S(1)} %collective-permute-done.2.zed_ref) | copy-start | bytes 393220
  27.2 0.8 %copy-start = (f32[512,128]{1,0:T(8,128)}, f32[512,128]{1,0:T(8,128)S(1)}, u32[]{:S(2)}) copy-start(f32[512,128]{1,0:T(8,128)S(1)} %collective-permute-done.fprev_ref) | copy-start | bytes 786436
  27.2 0.8 %copy-start.1 = (f32[512,128]{1,0:T(8,128)}, f32[512,128]{1,0:T(8,128)S(1)}, u32[]{:S(2)}) copy-start(f32[512,128]{1,0:T(8,128)S(1)} %collective-permute-done.1.fnext_ref) | copy-start | bytes 786436
